TPU v7x, 512 devices: a 4x2x32 block of a 4x8x32 slice. The times are simulated.
512 devices in a mesh: angle: 2 (over y), row: 128 (over z, x), col: 2 (over core).
Axes of the slice: x: 4, y: 2, z: 32, core: 2. Of those that a mesh axis runs over, the one named last changes fastest.
The devices are a block of a 4x8x32 slice.
Arguments:
- obj_field: float32 [2, 32768, 1024], P(None, ('angle', 'row'), 'col'), parts along dimension 1, may hold values from -6 to 6
- probe_modes: bfloat16 [2, 6, 256, 256], replicated, may hold values from -6 to 6
- centers: int32 [512, 2], P(('angle', 'row', 'col')), parts along dimension 0, may hold values from 0 to 16383, as said below
- amplitudes: float32 [512, 256, 256], P(('angle', 'row', 'col')), parts along dimension 0, may hold values from 0.2 to 4
Outputs:
- new_object: float32 [2, 32768, 1024], P(None, ('angle', 'row'), 'col'), parts along dimension 1
- new_probe: float32 [2, 12, 256, 256], P(None, 'angle'), parts along dimension 1
There are 2 independent parts, one for each index of `angle`. A program takes and returns all parts, laid end to end along the dimension named above; an argument that names none is the same for every part. Nothing has to cross between parts.
Inputs may be any that keep to these rules, and one draw needn't show every extreme that they name: `centers`: position k belongs to device d = k // 1 of the row+col order (row slowest); its centre lies in that device's tile: row in [(d // (1024 // 512)) * 128, + 128), column in [(d % (1024 // 512)) * 512, + 512).
All inputs are finite; a program needn't handle non-finite values.
Results may differ from a plain program's by a relative error of at most 0.0003.
Values sent between devices are 32-bit elements; how exact they have to be, the bound alone decides.
No kernel may reach another device: no remote copies, remote signals or barrier semaphores. Data moves between devices by JAX's collectives and lax.ppermute only.
A program may use at most 64 MiB of HBM per device.

v0:
```python
import functools
import math

import jax
import jax.numpy as jnp
import numpy as np
from jax import lax
from jax.experimental import pallas as pl
from jax.experimental.pallas import tpu as pltpu
from jax.sharding import Mesh
from jax.sharding import PartitionSpec as P


ROW = ("row_0", "row_1", "row_2")
ROW_COL = ROW + ("col",)
ANGLE_ROW = ("angle",) + ROW
ANGLE_ROW_COL = ANGLE_ROW + ("col",)
TILE = (8, 128)


def partners(row_step, swap):
    rows = math.prod(lax.axis_size(axis) for axis in ROW)
    cols = lax.axis_size("col")
    assert cols == 2
    return [
        (row * cols + col, (row + row_step) * cols + (1 - col if swap else col))
        for row in range(rows)
        for col in range(cols)
        if 0 <= row + row_step < rows
    ]


def extended_tile(block, margin):
    rows, cols = block.shape[1:]
    assert rows == margin
    left_col = lax.axis_index("col") == 0
    edge = jnp.where(left_col, block[:, :, cols - margin :], block[:, :, :margin])
    above = lax.ppermute(block, ROW_COL, partners(1, False))
    below = lax.ppermute(block, ROW_COL, partners(-1, False))
    edge_above = lax.ppermute(edge, ROW_COL, partners(1, True))
    edge_below = lax.ppermute(edge, ROW_COL, partners(-1, True))
    beside = lax.ppermute(edge, ROW_COL, partners(0, True))
    middle = jnp.concatenate([above, block, below], axis=1)
    side = jnp.concatenate([edge_above, beside, edge_below], axis=1)
    zero = jnp.zeros_like(side)
    return jnp.concatenate(
        [jnp.where(left_col, zero, side), middle, jnp.where(left_col, side, zero)], axis=2
    )


def place_kernel(start, column, stacked, up, own, down, side, buffer):
    channels, height, width = stacked.shape
    rows, cols = own.shape[1:]
    left_col = column[0] == 0
    shift = lax.rem(start[1], 128)
    where = pl.ds(pl.multiple_of(start[1] - shift, 128), width + 128)
    buffer[...] = jnp.zeros_like(buffer)

    @pl.loop(0, channels)
    def _(k):
        tall = jnp.concatenate([stacked[k], jnp.zeros((rows, width), jnp.float32)], axis=0)
        tall = pltpu.roll(tall, start[0], 0)
        wide = jnp.concatenate([tall, jnp.zeros((height + rows, 128), jnp.float32)], axis=1)
        buffer[:, where] = pltpu.roll(wide, shift, 1)
        up[k] = buffer[:rows, rows : rows + cols]
        own[k] = buffer[rows : 2 * rows, rows : rows + cols]
        down[k] = buffer[2 * rows :, rows : rows + cols]
        side[k] = jnp.where(left_col, buffer[:, rows + cols :], buffer[:, :rows])


def place(start, column, stacked, rows, cols):
    channels, height, width = stacked.shape
    assert height == width == 2 * rows and rows == 128
    smem = pl.BlockSpec(memory_space=pltpu.SMEM)
    vmem = pl.BlockSpec(memory_space=pltpu.VMEM)
    part = jax.ShapeDtypeStruct((channels, rows, cols), jnp.float32)
    return pl.pallas_call(
        place_kernel,
        name="place",
        out_shape=(part, part, part, jax.ShapeDtypeStruct((channels, 3 * rows, rows), jnp.float32)),
        in_specs=[smem, smem, vmem],
        out_specs=(vmem,) * 4,
        scratch_shapes=[pltpu.VMEM((3 * rows, cols + 2 * rows), jnp.float32)],
        compiler_params=pltpu.CompilerParams(vmem_limit_bytes=24 * 1024 * 1024),
        cost_estimate=pl.CostEstimate(
            flops=20 * part.size, bytes_accessed=24 * part.size, transcendentals=0
        ),
    )(start, column, stacked)


def folded_tile(pieces):
    up, own, down, side = pieces
    rows, cols = own.shape[1:]
    left_col = lax.axis_index("col") == 0
    got = lax.ppermute(side, ROW_COL, partners(0, True))
    rest = jnp.zeros(got.shape[:2] + (cols - rows,), got.dtype)
    got = jnp.where(
        left_col, jnp.concatenate([rest, got], axis=2), jnp.concatenate([got, rest], axis=2)
    )
    up, own, down = (
        piece + got[:, k * rows : (k + 1) * rows] for k, piece in enumerate((up, own, down))
    )
    from_below = lax.ppermute(up, ROW_COL, partners(-1, False))
    from_above = lax.ppermute(down, ROW_COL, partners(1, False))
    return own + from_below + from_above


def dft_tables(side):
    index = np.arange(side)
    phase = (index[:, None] * index[None, :] % side) * (2.0 * math.pi / side)
    cosine, sine = np.cos(phase) / math.sqrt(side), np.sin(phase) / math.sqrt(side)
    both = np.block([[cosine, sine], [-sine, cosine]])
    out = []
    for table in (both, both.T):
        head = table.astype(jnp.bfloat16)
        out.append((head, (table - head.astype(np.float64)).astype(jnp.bfloat16)))
    return out


def split(x):
    head = x.astype(jnp.bfloat16)
    return head, (x - head.astype(jnp.float32)).astype(jnp.bfloat16)


def right_dot(x, table):
    head, rest = split(x)
    return jnp.dot(
        jnp.concatenate([head, rest, head], axis=1),
        jnp.concatenate([table[0], table[0], table[1]], axis=0),
        preferred_element_type=jnp.float32,
    )


def left_dot(table, x):
    head, rest = split(x)
    return jnp.dot(
        jnp.concatenate([table[0], table[0], table[1]], axis=1),
        jnp.concatenate([head, rest, head], axis=0),
        preferred_element_type=jnp.float32,
    )


def wave_kernel(column, win, probe, amp, forward, inverse, obj, kept, sent, far, factor):
    modes, side = probe.shape[1], probe.shape[2]
    left_col = column[0] == 0
    tiles = side // 8

    def exit_wave(m):
        probe_real = probe[0, m].astype(jnp.float32)
        probe_imag = probe[1, m].astype(jnp.float32)
        exit_real = probe_real * win[0] - probe_imag * win[1]
        exit_imag = probe_real * win[1] + probe_imag * win[0]
        return probe_real, probe_imag, exit_real, exit_imag

    def transform(real, imag, right, left):
        mixed = right_dot(jnp.concatenate([real, imag], axis=1), right)
        return left_dot(left, jnp.concatenate([mixed[:, :side], mixed[:, side:]], axis=0))

    def put(base, first, second):
        where = pl.ds(base, tiles)
        kept[where] = jnp.where(left_col, first, second).reshape((tiles,) + TILE)
        sent[where] = jnp.where(left_col, second, first).reshape((tiles,) + TILE)

    factor[...] = jnp.zeros_like(factor)

    @pl.loop(0, modes)
    def _(m):
        _, _, exit_real, exit_imag = exit_wave(m)
        out = transform(exit_real, exit_imag, inverse, forward)
        far[m] = out
        factor[...] += out[:side] * out[:side] + out[side:] * out[side:]

    factor[...] = amp[...] / (jnp.sqrt(factor[...]) + 0.5)
    obj[...] = jnp.zeros_like(obj)

    @pl.loop(0, modes)
    def _(m):
        scale = factor[...]
        back = transform(far[m, :side] * scale, far[m, side:] * scale, forward, inverse)
        probe_real, probe_imag, exit_real, exit_imag = exit_wave(m)
        diff_real = back[:side] - exit_real
        diff_imag = back[side:] - exit_imag
        obj[0] += probe_real * diff_real + probe_imag * diff_imag
        obj[1] += probe_real * diff_imag - probe_imag * diff_real
        obj[2] += probe_real * probe_real + probe_imag * probe_imag
        grad_real = win[0] * diff_real + win[1] * diff_imag
        grad_imag = win[0] * diff_imag - win[1] * diff_real
        for half in range(side // 128):
            cols = slice(128 * half, 128 * half + 128)
            put((m * (side // 128) + half) * tiles, grad_real[:, cols], grad_imag[:, cols])

    weight = win[0] * win[0] + win[1] * win[1]
    put(modes * (side // 128) * tiles, weight[:, :128], weight[:, 128:])


def waves(column, window, probe, amplitude):
    modes, side = probe.shape[1], probe.shape[2]
    assert side == 256
    forward, inverse = (jnp.asarray(np.stack(table)) for table in dft_tables(side))
    flops = 4 * modes * 2 * side * (6 * side) * (2 * side)
    half = jax.ShapeDtypeStruct(((2 * modes + 1) * (side // 8),) + TILE, jnp.float32)
    vmem = pl.BlockSpec(memory_space=pltpu.VMEM)
    return pl.pallas_call(
        wave_kernel,
        name="waves",
        out_shape=(jax.ShapeDtypeStruct((3, side, side), jnp.float32), half, half),
        in_specs=[pl.BlockSpec(memory_space=pltpu.SMEM)] + [vmem] * 5,
        out_specs=(vmem, vmem, vmem),
        scratch_shapes=[
            pltpu.VMEM((modes, 2 * side, side), jnp.float32),
            pltpu.VMEM((side, side), jnp.float32),
        ],
        compiler_params=pltpu.CompilerParams(vmem_limit_bytes=40 * 1024 * 1024),
        cost_estimate=pl.CostEstimate(
            flops=flops, bytes_accessed=12 * 1024 * 1024, transcendentals=0
        ),
    )(column, window, probe, amplitude, forward, inverse)


def probe_kernel(column, own, other, probe, out):
    modes, side = probe.shape[1], probe.shape[2]
    left_col = column[0] == 0
    chunk = own.shape[1] - 1
    group = math.gcd(chunk, side // 8)

    def halves(tile):
        where = (tile // chunk, slice(tile % chunk, tile % chunk + group))
        mine, theirs = (ref[where].reshape(8 * group, 128) for ref in (own, other))
        return jnp.where(left_col, mine, theirs), jnp.where(left_col, theirs, mine)

    per_half = side // 8
    groups = per_half // group
    base = 2 * modes * per_half
    weight = [halves(base + j * group) for j in range(groups)]
    peak = functools.reduce(jnp.maximum, [jnp.max(w) for pair in weight for w in pair])
    for j in range(groups):
        rows = slice(8 * group * j, 8 * group * (j + 1))
        for half in range(2):
            inverse = 1.0 / (weight[j][half] + 0.1 * peak)
            cols = slice(128 * half, 128 * half + 128)
            for m in range(modes):
                grads = halves((2 * m + half) * per_half + j * group)
                for part in range(2):
                    out[part, m, rows, cols] = (
                        probe[part, m, rows, cols].astype(jnp.float32) + grads[part] * inverse
                    )


def probe_update(column, own, other, probe):
    vmem = pl.BlockSpec(memory_space=pltpu.VMEM)
    return pl.pallas_call(
        probe_kernel,
        name="probe_update",
        out_shape=jax.ShapeDtypeStruct(probe.shape, jnp.float32),
        in_specs=[pl.BlockSpec(memory_space=pltpu.SMEM)] + [vmem] * 3,
        out_specs=vmem,
        compiler_params=pltpu.CompilerParams(vmem_limit_bytes=40 * 1024 * 1024),
        cost_estimate=pl.CostEstimate(
            flops=4 * probe.size, bytes_accessed=9 * probe.size, transcendentals=0
        ),
    )(column, own, other, probe)


def exchange(chunks, axis):
    return lax.all_to_all(chunks, axis, 0, 0, tiled=True)


def scatter_sum(tiles, axis):
    count = lax.axis_size(axis)
    part = -(-tiles.shape[0] // count)
    tiles = jnp.pad(tiles, ((0, part * count - tiles.shape[0]), (0, 0), (0, 0)))
    return jnp.sum(exchange(tiles.reshape((count, part) + TILE), axis), axis=0)


def gather(tiles, peak, axis):
    count = lax.axis_size(axis)
    tagged = jnp.concatenate([tiles, peak])
    return exchange(jnp.broadcast_to(tagged, (count,) + tagged.shape), axis)


def sum_and_peak(kept, sent, local_peak):
    swap = [(0, 1), (1, 0)]
    tiles = kept + lax.ppermute(sent, "col", swap)
    counts = []
    for axis in ROW[::-1]:
        counts.append(tiles.shape[0])
        tiles = scatter_sum(tiles, axis)
    peak = jnp.full((1,) + TILE, local_peak)
    for axis, count in zip(ROW, counts[::-1], strict=True):
        got = gather(tiles, peak, axis)
        peak = jnp.max(got[:, -1:], axis=0)
        tiles = got[:, :-1].reshape((-1,) + TILE)[:count]
    other = lax.ppermute(got, "col", swap)
    peak = jnp.maximum(peak, jnp.max(other[:, -1:], axis=0))
    return got, other, peak[0, 0, 0]


def update(obj_field, probe_modes, centers, amplitudes):
    tile_rows, tile_cols = obj_field.shape[1:]
    side = probe_modes.shape[2]
    margin = side // 2
    start_row = centers[0, 0] - lax.axis_index(ROW) * tile_rows
    start_col = centers[0, 1] - lax.axis_index("col") * tile_cols
    zero = jnp.zeros((), jnp.int32)
    column = lax.axis_index("col").astype(jnp.int32).reshape(1)
    extended = extended_tile(obj_field, margin)
    window = lax.dynamic_slice(extended, (zero, start_row, start_col), (2, side, side))
    stacked, kept, sent = waves(column, window, probe_modes, amplitudes[0])
    start = jnp.stack([start_row, start_col])
    folded = folded_tile(place(start, column, stacked, tile_rows, tile_cols))
    illumination = folded[2]
    own, other, peak = sum_and_peak(kept, sent, jnp.max(illumination))
    new_object = obj_field + folded[:2] / (illumination + 0.1 * peak)
    return new_object, probe_update(column, own, other, probe_modes)


def solution(mesh):
    near, middle = 4, min(4, mesh.shape["row"] // 4)
    rows = mesh.shape["row"]
    split_mesh = Mesh(
        mesh.devices.reshape(
            mesh.shape["angle"], rows // (near * middle), middle, near, mesh.shape["col"]
        ),
        ANGLE_ROW_COL,
    )
    return jax.shard_map(
        update,
        mesh=split_mesh,
        in_specs=(
            P(None, ANGLE_ROW, "col"),
            P(),
            P(ANGLE_ROW_COL, None),
            P(ANGLE_ROW_COL, None, None),
        ),
        out_specs=(P(None, ANGLE_ROW, "col"), P(None, "angle", None, None)),
        check_vma=False,
    )
```

profile of v0, /device:TPU:40, one launch (start us, length us, event | category | flops | bytes accessed | tf_op | source)
XLA Modules:
  0.0 267.6 jit_solution(1337413716529319785)
XLA Ops:
  0.6 0.0 copy-start.5
  0.6 1.0 slice_select_fusion
  1.7 3.1 %collective-permute-start = (f32[2,128,128]{2,1,0:T(8,128)S(1)}, f32[2,128,128]{2,1,0:T(8,128)S(1)}, u32[]{:S(2)}, u32[]{:S(2)}) collective-permute-start(f32[2,128,128]{2,1,0:T(8,128)S(1)} %slice_select_fusion), channel_id=1, source_target_pairs={{0,3},{1,2},{2,5},{3,4},{4,7},{5,6},{6,9},{7,8},{8,11},{9,10},{10,... | collective-permute-start | bytes 393224 | tf_op jit(solution)/shard_map/ppermute | solution.py:40
  4.8 2.5 collective-permute-start.1
  7.3 1.3 collective-permute-start.2
  8.7 4.2 %collective-permute-start.3 = (f32[2,128,512]{2,1,0:T(8,128)}, f32[2,128,512]{2,1,0:T(8,128)S(1)}, u32[]{:S(2)}, u32[]{:S(2)}) collective-permute-start(f32[2,128,512]{2,1,0:T(8,128)} %param.6), channel_id=1, source_target_pairs={{0,2},{1,3},{2,4},{3,5},{4,6},{5,7},{6,8},{7,9},{8,10},{9,11},{10,... | collective-permute-start | bytes 1572872 | tf_op jit(solution)/shard_map/ppermute | solution.py:38
  12.9 1.3 collective-permute-start.4
  14.2 1.3 fusion.7
  16.9 0.0 copy-start.1
  16.9 0.0 copy-start.2
  16.9 0.0 copy-start.3
  16.9 1.1 constant_dynamic-update-slice_fusion.1
  18.0 0.1 broadcast_select_fusion
  18.1 6.9 %collective-permute-done.3 = f32[2,128,512]{2,1,0:T(8,128)S(1)} collective-permute-done((f32[2,128,512]{2,1,0:T(8,128)}, f32[2,128,512]{2,1,0:T(8,128)S(1)}, u32[]{:S(2)}, u32[]{:S(2)}) %collective-permute-start.3) | collective-permute-done | bytes 524320 | tf_op jit(solution)/shard_map/ppermute | solution.py:38
  25.0 4.2 %collective-permute-done.4 = f32[2,128,512]{2,1,0:T(8,128)} collective-permute-done((f32[2,128,512]{2,1,0:T(8,128)}, f32[2,128,512]{2,1,0:T(8,128)}, u32[]{:S(2)}, u32[]{:S(2)}) %collective-permute-start.4) | collective-permute-done | bytes 524320 | tf_op jit(solution)/shard_map/ppermute | solution.py:39
  29.2 1.5 fusion.3.win
  30.8 14.6 %waves.1 = (f32[3,256,256]{2,1,0:T(8,128)S(1)}, f32[416,8,128]{2,1,0:T(8,128)S(1)}, f32[416,8,128]{2,1,0:T(8,128)S(1)}) custom-call(s32[1]{0:T(128)} %bitcast.4.column, f32[2,256,256]{2,1,0:T(8,128)S(1)} %fusion.3.win, bf16[2,6,256,256]{3,2,1,0:T(8,128)(2,1)S(1)} %copy-done, f32[256,256]{1,0:T(8,128)S(1)} %bitcast.18, bf16[2,512,512]{2,1,0:T(8,128)(2,1)S(1)} %copy-done.2, ...), custom_call_target="tpu_custom_call" | custom-call | flops 9663676416 | bytes 12582912 | tf_op jit(solution)/shard_map/waves/pallas_call | solution.py:203
  45.4 2.0 collective-permute-start.8
  47.4 3.6 %collective-permute-done.8 = f32[416,8,128]{2,1,0:T(8,128)S(1)} collective-permute-done((f32[416,8,128]{2,1,0:T(8,128)S(1)}, f32[416,8,128]{2,1,0:T(8,128)S(1)}, u32[]{:S(2)}, u32[]{:S(2)}) %collective-permute-start.8) | collective-permute-done | bytes 1703968 | tf_op jit(solution)/shard_map/ppermute | solution.py:283
  51.0 0.2 add.57
  51.1 31.7 %all_to_all.30 = f32[4,104,8,128]{3,2,1,0:T(8,128)} all-to-all(f32[4,104,8,128]{3,2,1,0:T(8,128)S(1)} %bitcast.19), channel_id=1, replica_groups=mesh['angle'=2,'row_0'=8,'row_1'=4,'row_2'=4,'col'=2] {'row_2'}, dimensions={0} | all-to-all | bytes 3407872 | tf_op jit(solution)/shard_map/all_to_all | solution.py:265
  82.9 2.3 reduce_sum.27
  85.2 12.0 %all-to-all-start.1 = ((f32[4,26,8,128]{3,2,1,0:T(8,128)}), f32[4,26,8,128]{3,2,1,0:T(8,128)}, u32[]{:S(2)}, u32[]{:S(2)}) async-start(f32[4,26,8,128]{3,2,1,0:T(8,128)} %bitcast.7), calls=%async_computation.1 | async-start | bytes 851968 | tf_op jit(solution)/shard_map/all_to_all | solution.py:265
  97.2 0.1 pad_add_fusion.start
  97.3 1.7 place.1
  99.0 2.0 collective-permute-start.5
  101.0 2.0 collective-permute-done.5
  102.9 0.3 pad_select_fusion
  103.3 1.5 slice_add_fusion.1
  104.8 0.2 copy-done.4
  104.9 1.3 collective-permute-start.6
  106.2 5.5 %collective-permute-start.7 = (f32[3,128,512]{2,1,0:T(8,128)S(1)}, f32[3,128,512]{2,1,0:T(8,128)}, u32[]{:S(2)}, u32[]{:S(2)}) collective-permute-start(f32[3,128,512]{2,1,0:T(8,128)S(1)} %get-tuple-element.17), channel_id=1, source_target_pairs={{0,2},{1,3},{2,4},{3,5},{4,6},{5,7},{6,8},{7,9},{8,10},{9,11},{10,... | collective-permute-start | bytes 2359304 | tf_op jit(solution)/shard_map/ppermute | solution.py:104
  111.7 1.0 reduce_sum.28
  112.8 0.7 pad.7
  113.4 37.3 %all-to-all-start.2 = ((f32[8,4,8,128]{3,2,1,0:T(8,128)}), f32[8,4,8,128]{3,2,1,0:T(8,128)S(1)}, u32[]{:S(2)}, u32[]{:S(2)}) async-start(f32[8,4,8,128]{3,2,1,0:T(8,128)} %bitcast.8), calls=%async_computation.2 | async-start | bytes 262144 | tf_op jit(solution)/shard_map/all_to_all | solution.py:265
  150.8 2.0 fusion.1
  152.7 0.7 slice_reduce_fusion
  153.4 27.9 %all-to-all-done.2 = f32[8,4,8,128]{3,2,1,0:T(8,128)S(1)} async-done(((f32[8,4,8,128]{3,2,1,0:T(8,128)}), f32[8,4,8,128]{3,2,1,0:T(8,128)S(1)}, u32[]{:S(2)}, u32[]{:S(2)}) %all-to-all-start.2) | async-done | bytes 131104 | tf_op jit(solution)/shard_map/all_to_all | solution.py:265
  181.3 0.7 concatenate.29
  182.0 36.2 %all_to_all.31 = f32[8,5,8,128]{3,2,1,0:T(8,128)S(1)} all-to-all(f32[8,5,8,128]{3,2,1,0:T(8,128)S(1)} %broadcast_in_dim.16), channel_id=1, replica_groups=mesh['angle'=2,'row_0'=8,'row_1'=4,'row_2'=4,'col'=2] {'row_0'}, dimensions={0} | all-to-all | bytes 327680 | tf_op jit(solution)/shard_map/all_to_all | solution.py:265
  218.3 14.5 %all_to_all.32 = f32[4,27,8,128]{3,2,1,0:T(8,128)S(1)} all-to-all(f32[4,27,8,128]{3,2,1,0:T(8,128)S(1)} %broadcast_in_dim.17), channel_id=1, replica_groups=mesh['angle'=2,'row_0'=8,'row_1'=4,'row_2'=4,'col'=2] {'row_1'}, dimensions={0} | all-to-all | bytes 884736 | tf_op jit(solution)/shard_map/all_to_all | solution.py:265
  232.9 0.1 broadcast_in_dim.18
  233.1 24.6 %all_to_all.33.own = f32[4,105,8,128]{3,2,1,0:T(8,128)S(1)} all-to-all(f32[4,105,8,128]{3,2,1,0:T(8,128)S(1)} %broadcast_in_dim.18), channel_id=1, replica_groups=mesh['angle'=2,'row_0'=8,'row_1'=4,'row_2'=4,'col'=2] {'row_2'}, dimensions={0} | all-to-all | bytes 3440640 | tf_op jit(solution)/shard_map/all_to_all | solution.py:265
  257.7 1.9 collective-permute-start.9
  259.6 3.6 %collective-permute-done.9.other = f32[4,105,8,128]{3,2,1,0:T(8,128)S(1)} collective-permute-done((f32[4,105,8,128]{3,2,1,0:T(8,128)S(1)}, f32[4,105,8,128]{3,2,1,0:T(8,128)S(1)}, u32[]{:S(2)}, u32[]{:S(2)}) %collective-permute-start.9) | collective-permute-done | bytes 1720352 | tf_op jit(solution)/shard_map/ppermute | solution.py:293
  263.2 0.5 slice.67
  264.4 0.9 fusion.6
  265.3 2.2 probe_update.1
  (31 shorter events, 0.3 us)
Async XLA Ops:
  0.6 28.6 %copy-start.5 = (f32[2,128,512]{2,1,0:T(8,128)S(1)}, f32[2,128,512]{2,1,0:T(8,128)}, u32[]{:S(2)}) copy-start(f32[2,128,512]{2,1,0:T(8,128)} %param.6) | copy-start | bytes 1572868
  1.7 15.2 %collective-permute-start = (f32[2,128,128]{2,1,0:T(8,128)S(1)}, f32[2,128,128]{2,1,0:T(8,128)S(1)}, u32[]{:S(2)}, u32[]{:S(2)}) collective-permute-start(f32[2,128,128]{2,1,0:T(8,128)S(1)} %slice_select_fusion), channel_id=1, source_target_pairs={{0,3},{1,2},{2,5},{3,4},{4,7},{5,6},{6,9},{7,8},{8,11},{9,10},{10,... | collective-permute-start | bytes 393224 | tf_op jit(solution)/shard_map/ppermute | solution.py:40
  4.8 12.1 %collective-permute-start.1 = (f32[2,128,128]{2,1,0:T(8,128)S(1)}, f32[2,128,128]{2,1,0:T(8,128)}, u32[]{:S(2)}, u32[]{:S(2)}) collective-permute-start(f32[2,128,128]{2,1,0:T(8,128)S(1)} %slice_select_fusion), channel_id=1, source_target_pairs={{0,1},{1,0},{2,3},{3,2},{4,5},{5,4},{6,7},{7,6},{8,9},{9,8},{10,11... | collective-permute-start | bytes 393224 | tf_op jit(solution)/shard_map/ppermute | solution.py:42
  7.3 10.7 %collective-permute-start.2 = (f32[2,128,128]{2,1,0:T(8,128)S(1)}, f32[2,128,128]{2,1,0:T(8,128)S(1)}, u32[]{:S(2)}, u32[]{:S(2)}) collective-permute-start(f32[2,128,128]{2,1,0:T(8,128)S(1)} %slice_select_fusion), channel_id=1, source_target_pairs={{2,1},{3,0},{4,3},{5,2},{6,5},{7,4},{8,7},{9,6},{10,9},{11,8},{12,... | collective-permute-start | bytes 393224 | tf_op jit(solution)/shard_map/ppermute | solution.py:41
  8.7 16.4 %collective-permute-start.3 = (f32[2,128,512]{2,1,0:T(8,128)}, f32[2,128,512]{2,1,0:T(8,128)S(1)}, u32[]{:S(2)}, u32[]{:S(2)}) collective-permute-start(f32[2,128,512]{2,1,0:T(8,128)} %param.6), channel_id=1, source_target_pairs={{0,2},{1,3},{2,4},{3,5},{4,6},{5,7},{6,8},{7,9},{8,10},{9,11},{10,... | collective-permute-start | bytes 1572872 | tf_op jit(solution)/shard_map/ppermute | solution.py:38
  12.9 16.3 %collective-permute-start.4 = (f32[2,128,512]{2,1,0:T(8,128)}, f32[2,128,512]{2,1,0:T(8,128)}, u32[]{:S(2)}, u32[]{:S(2)}) collective-permute-start(f32[2,128,512]{2,1,0:T(8,128)} %param.6), channel_id=1, source_target_pairs={{2,0},{3,1},{4,2},{5,3},{6,4},{7,5},{8,6},{9,7},{10,8},{11,9},{12,... | collective-permute-start | bytes 1572872 | tf_op jit(solution)/shard_map/ppermute | solution.py:39
  16.9 13.9 %copy-start = (bf16[2,6,256,256]{3,2,1,0:T(8,128)(2,1)S(1)}, bf16[2,6,256,256]{3,2,1,0:T(8,128)(2,1)}, u32[]{:S(2)}) copy-start(bf16[2,6,256,256]{3,2,1,0:T(8,128)(2,1)} %probe.3) | copy-start | bytes 4718596
  16.9 13.9 %copy-start.1 = (f32[1,256,256]{2,1,0:T(8,128)S(1)}, f32[1,256,256]{2,1,0:T(8,128)}, u32[]{:S(2)}) copy-start(f32[1,256,256]{2,1,0:T(8,128)} %param.9) | copy-start | bytes 786436
  16.9 13.9 %copy-start.2 = (bf16[2,512,512]{2,1,0:T(8,128)(2,1)S(1)}, bf16[2,512,512]{2,1,0:T(8,128)(2,1)}, u32[]{:S(2)}) copy-start(bf16[2,512,512]{2,1,0:T(8,128)(2,1)} %constant.44.clone.forward) | copy-start | bytes 3145732
  16.9 13.9 %copy-start.3 = (bf16[2,512,512]{2,1,0:T(8,128)(2,1)S(1)}, bf16[2,512,512]{2,1,0:T(8,128)(2,1)}, u32[]{:S(2)}) copy-start(bf16[2,512,512]{2,1,0:T(8,128)(2,1)} %constant.45.clone.inverse) | copy-start | bytes 3145732
  45.4 5.5 %collective-permute-start.8 = (f32[416,8,128]{2,1,0:T(8,128)S(1)}, f32[416,8,128]{2,1,0:T(8,128)S(1)}, u32[]{:S(2)}, u32[]{:S(2)}) collective-permute-start(f32[416,8,128]{2,1,0:T(8,128)S(1)} %get-tuple-element.15), channel_id=1, source_target_pairs={{0,1},{1,0},{2,3},{3,2},{4,5},{5,4},{6,7},{7,6},{8,9},{9,8},{10,11... | collective-permute-start | bytes 5111816 | tf_op jit(solution)/shard_map/ppermute | solution.py:283
  85.2 26.5 %all-to-all-start.1 = ((f32[4,26,8,128]{3,2,1,0:T(8,128)}), f32[4,26,8,128]{3,2,1,0:T(8,128)}, u32[]{:S(2)}, u32[]{:S(2)}) async-start(f32[4,26,8,128]{3,2,1,0:T(8,128)} %bitcast.7), calls=%async_computation.1 | async-start | bytes 851968 | tf_op jit(solution)/shard_map/all_to_all | solution.py:265
  99.0 3.9 %collective-permute-start.5 = (f32[3,384,128]{2,1,0:T(8,128)S(1)}, f32[3,384,128]{2,1,0:T(8,128)S(1)}, u32[]{:S(2)}, u32[]{:S(2)}) collective-permute-start(f32[3,384,128]{2,1,0:T(8,128)S(1)} %get-tuple-element.11), channel_id=1, source_target_pairs={{0,1},{1,0},{2,3},{3,2},{4,5},{5,4},{6,7},{7,6},{8,9},{9,8},{10,11... | collective-permute-start | bytes 1769480 | tf_op jit(solution)/shard_map/ppermute | solution.py:95
  103.3 1.7 copy-start.4
  104.9 45.8 %collective-permute-start.6 = (f32[3,128,512]{2,1,0:T(8,128)}, f32[3,128,512]{2,1,0:T(8,128)}, u32[]{:S(2)}, u32[]{:S(2)}) collective-permute-start(f32[3,128,512]{2,1,0:T(8,128)} %get-tuple-element.16), channel_id=1, source_target_pairs={{2,0},{3,1},{4,2},{5,3},{6,4},{7,5},{8,6},{9,7},{10,8},{11,9},{12,... | collective-permute-start | bytes 2359304 | tf_op jit(solution)/shard_map/ppermute | solution.py:103
  106.2 44.5 %collective-permute-start.7 = (f32[3,128,512]{2,1,0:T(8,128)S(1)}, f32[3,128,512]{2,1,0:T(8,128)}, u32[]{:S(2)}, u32[]{:S(2)}) collective-permute-start(f32[3,128,512]{2,1,0:T(8,128)S(1)} %get-tuple-element.17), channel_id=1, source_target_pairs={{0,2},{1,3},{2,4},{3,5},{4,6},{5,7},{6,8},{7,9},{8,10},{9,11},{10,... | collective-permute-start | bytes 2359304 | tf_op jit(solution)/shard_map/ppermute | solution.py:104
  113.4 67.9 %all-to-all-start.2 = ((f32[8,4,8,128]{3,2,1,0:T(8,128)}), f32[8,4,8,128]{3,2,1,0:T(8,128)S(1)}, u32[]{:S(2)}, u32[]{:S(2)}) async-start(f32[8,4,8,128]{3,2,1,0:T(8,128)} %bitcast.8), calls=%async_computation.2 | async-start | bytes 262144 | tf_op jit(solution)/shard_map/all_to_all | solution.py:265
  233.0 31.4 %copy-start.6 = (f32[2,128,512]{2,1,0:T(8,128)S(1)}, f32[2,128,512]{2,1,0:T(8,128)}, u32[]{:S(2)}) copy-start(f32[2,128,512]{2,1,0:T(8,128)} %param.6) | copy-start | bytes 1572868
  257.7 5.5 %collective-permute-start.9 = (f32[4,105,8,128]{3,2,1,0:T(8,128)S(1)}, f32[4,105,8,128]{3,2,1,0:T(8,128)S(1)}, u32[]{:S(2)}, u32[]{:S(2)}) collective-permute-start(f32[4,105,8,128]{3,2,1,0:T(8,128)S(1)} %all_to_all.33.own), channel_id=1, source_target_pairs={{0,1},{1,0},{2,3},{3,2},{4,5},{5,4},{6,7},{7,6},{8,9},{9,8},{10,11... | collective-permute-start | bytes 5160968 | tf_op jit(solution)/shard_map/ppermute | solution.py:293
where the time goes:
time: 270 us; the launch traced here: 268 us
  blocking collectives  107 us (40%)
  starting transfers between devices  74.4 us (28%)
  waiting for transfers between devices  48.2 us (18%)
  Pallas kernels  18.6 us (7%)
  other arithmetic  11.7 us (4%)
  local copies, waits for them, and re-layouts  4.64 us (2%)
  between operations  2.98 us (1%)
    all_to_all x4, blocking collectives, exchange(): return lax.all_to_all(chunks, axis, 0, 0, tiled=True)  107 us
    all_to_all x2, starting transfers between devices, exchange(): return lax.all_to_all(chunks, axis, 0, 0, tiled=True)  49.3 us
    all_to_all x2, waiting for transfers between devices, exchange(): return lax.all_to_all(chunks, axis, 0, 0, tiled=True)  27.9 us
    pallas_call x1, Pallas kernels, waves(): pl.pallas_call(wave_kernel, name='waves', out_shape=(jax.ShapeDtypeStruct...  14.6 us
    ppermute x1, waiting for transfers between devices, extended_tile(): above = lax.ppermute(block, ROW_COL, partners(1, False))  6.92 us
    ppermute x1, starting transfers between devices, folded_tile(): from_above = lax.ppermute(down, ROW_COL, partners(1, False))  5.5 us
  transfers between devices with their start and end apart: 12, of which 6 were waited for; matrix products, arithmetic and copies ran while one was open for 3% of the time, Pallas kernels for 1%

commit v1 on v0

--- a/solution.py
+++ b/solution.py
@@ -11,10 +11,11 @@
 from jax.sharding import PartitionSpec as P
 
 
-ROW = ("row_0", "row_1", "row_2")
+ROW = ("row_0", "row_1")
 ROW_COL = ROW + ("col",)
 ANGLE_ROW = ("angle",) + ROW
 ANGLE_ROW_COL = ANGLE_ROW + ("col",)
+NEAR = 8
 TILE = (8, 128)
 
 
@@ -265,34 +266,22 @@
     return lax.all_to_all(chunks, axis, 0, 0, tiled=True)
 
 
-def scatter_sum(tiles, axis):
-    count = lax.axis_size(axis)
-    part = -(-tiles.shape[0] // count)
-    tiles = jnp.pad(tiles, ((0, part * count - tiles.shape[0]), (0, 0), (0, 0)))
-    return jnp.sum(exchange(tiles.reshape((count, part) + TILE), axis), axis=0)
-
-
-def gather(tiles, peak, axis):
-    count = lax.axis_size(axis)
-    tagged = jnp.concatenate([tiles, peak])
-    return exchange(jnp.broadcast_to(tagged, (count,) + tagged.shape), axis)
-
-
 def sum_and_peak(kept, sent, local_peak):
+    far, near = (lax.axis_size(axis) for axis in ROW)
     swap = [(0, 1), (1, 0)]
     tiles = kept + lax.ppermute(sent, "col", swap)
-    counts = []
-    for axis in ROW[::-1]:
-        counts.append(tiles.shape[0])
-        tiles = scatter_sum(tiles, axis)
-    peak = jnp.full((1,) + TILE, local_peak)
-    for axis, count in zip(ROW, counts[::-1], strict=True):
-        got = gather(tiles, peak, axis)
-        peak = jnp.max(got[:, -1:], axis=0)
-        tiles = got[:, :-1].reshape((-1,) + TILE)[:count]
-    other = lax.ppermute(got, "col", swap)
-    peak = jnp.maximum(peak, jnp.max(other[:, -1:], axis=0))
-    return got, other, peak[0, 0, 0]
+    tiles = tiles.reshape((near, tiles.shape[0] // near) + TILE)
+    tiles = jnp.sum(exchange(tiles, "row_1"), axis=0)
+    part = tiles.shape[0] * TILE[0] // far
+    rows = jnp.sum(exchange(tiles.reshape(far, part, 128), "row_0"), axis=0)
+    spare = jnp.full((TILE[0] - part % TILE[0], 128), local_peak)
+    rows = jnp.concatenate([rows, spare])
+    got = exchange(jnp.broadcast_to(rows, (far,) + rows.shape), "row_0")
+    peak = jnp.full((1,) + TILE, jnp.max(got[:, part:]))
+    tiles = jnp.concatenate([got[:, :part].reshape(tiles.shape), peak])
+    own = exchange(jnp.broadcast_to(tiles, (near,) + tiles.shape), "row_1")
+    other = lax.ppermute(own, "col", swap)
+    return own, other, jnp.maximum(jnp.max(own[:, -1]), jnp.max(other[:, -1]))
 
 
 def update(obj_field, probe_modes, centers, amplitudes):
@@ -315,11 +304,9 @@
 
 
 def solution(mesh):
-    near, middle = 4, min(4, mesh.shape["row"] // 4)
-    rows = mesh.shape["row"]
     split_mesh = Mesh(
         mesh.devices.reshape(
-            mesh.shape["angle"], rows // (near * middle), middle, near, mesh.shape["col"]
+            mesh.shape["angle"], mesh.shape["row"] // NEAR, NEAR, mesh.shape["col"]
         ),
         ANGLE_ROW_COL,
     )

time: 270 us -> 274 us (1.015)
  blocking collectives: 107 us -> 92.5 us
  waiting for transfers between devices: 48.2 us -> 57.2 us
  starting transfers between devices: 74.4 us -> 80.5 us
    ppermute x1, waiting for transfers between devices: 0.01 us -> 14.8 us  [folded_tile(): from_below = lax.ppermute(up, ROW_COL, partners(-1, False))]
    all_to_all x4 -> x2, blocking collectives: 107 us -> 92.5 us  [exchange(): return lax.all_to_all(chunks, axis, 0, 0, tiled=True)]
    all_to_all x2, starting transfers between devices: 49.3 us -> 56.3 us  [exchange(): return lax.all_to_all(chunks, axis, 0, 0, tiled=True)]
    all_to_all x2, waiting for transfers between devices: 27.9 us -> 22.5 us  [exchange(): return lax.all_to_all(chunks, axis, 0, 0, tiled=True)]
  transfers between devices with their start and end apart: 12 -> 12, of which waited for: 6 -> 8; matrix products, arithmetic and copies ran while one was open for 3% -> 3% of each run, Pallas kernels for 1% -> 1%
where the time goes in v1:
time: 274 us; the launch traced here: 270 us
  blocking collectives  92.5 us (34%)
  starting transfers between devices  80.5 us (29%)
  waiting for transfers between devices  57.2 us (21%)
  Pallas kernels  19.4 us (7%)
  other arithmetic  12.8 us (5%)
  local copies, waits for them, and re-layouts  4.48 us (2%)
  between operations  3.61 us (1%)
    all_to_all x2, blocking collectives, exchange(): return lax.all_to_all(chunks, axis, 0, 0, tiled=True)  92.5 us
    all_to_all x2, starting transfers between devices, exchange(): return lax.all_to_all(chunks, axis, 0, 0, tiled=True)  56.3 us
    all_to_all x2, waiting for transfers between devices, exchange(): return lax.all_to_all(chunks, axis, 0, 0, tiled=True)  22.5 us
    ppermute x1, waiting for transfers between devices, folded_tile(): from_below = lax.ppermute(up, ROW_COL, partners(-1, False))  14.8 us
    pallas_call x1, Pallas kernels, waves(): pl.pallas_call(wave_kernel, name='waves', out_shape=(jax.ShapeDtypeStruct...  14.7 us
    ppermute x1, waiting for transfers between devices, extended_tile(): above = lax.ppermute(block, ROW_COL, partners(1, False))  7.97 us
  transfers between devices with their start and end apart: 12, of which 8 were waited for; matrix products, arithmetic and copies ran while one was open for 3% of the time, Pallas kernels for 1%

profile of v1, /device:TPU:40, one launch (start us, length us, event | category | flops | bytes accessed | tf_op | source)
XLA Modules:
  0.0 270.5 jit_solution(10585849882451499777)
XLA Ops:
  0.6 1.0 slice_select_fusion
  1.7 3.1 %collective-permute-start = (f32[2,128,128]{2,1,0:T(8,128)S(1)}, f32[2,128,128]{2,1,0:T(8,128)S(1)}, u32[]{:S(2)}, u32[]{:S(2)}) collective-permute-start(f32[2,128,128]{2,1,0:T(8,128)S(1)} %slice_select_fusion), channel_id=1, source_target_pairs={{0,3},{1,2},{2,5},{3,4},{4,7},{5,6},{6,9},{7,8},{8,11},{9,10},{10,... | collective-permute-start | bytes 393224 | tf_op jit(solution)/shard_map/ppermute | solution.py:41
  4.8 2.5 collective-permute-start.1
  7.3 1.3 collective-permute-start.2
  8.6 4.2 %collective-permute-start.3 = (f32[2,128,512]{2,1,0:T(8,128)}, f32[2,128,512]{2,1,0:T(8,128)S(1)}, u32[]{:S(2)}, u32[]{:S(2)}) collective-permute-start(f32[2,128,512]{2,1,0:T(8,128)} %param.6), channel_id=1, source_target_pairs={{0,2},{1,3},{2,4},{3,5},{4,6},{5,7},{6,8},{7,9},{8,10},{9,11},{10,... | collective-permute-start | bytes 1572872 | tf_op jit(solution)/shard_map/ppermute | solution.py:39
  12.9 1.3 collective-permute-start.4
  14.2 1.3 fusion.7
  16.9 0.0 copy-start.3
  16.9 0.0 copy-start.4
  17.0 0.1 broadcast_select_fusion
  17.0 8.0 %collective-permute-done.3 = f32[2,128,512]{2,1,0:T(8,128)S(1)} collective-permute-done((f32[2,128,512]{2,1,0:T(8,128)}, f32[2,128,512]{2,1,0:T(8,128)S(1)}, u32[]{:S(2)}, u32[]{:S(2)}) %collective-permute-start.3) | collective-permute-done | bytes 524320 | tf_op jit(solution)/shard_map/ppermute | solution.py:39
  25.0 4.1 %collective-permute-done.4 = f32[2,128,512]{2,1,0:T(8,128)S(1)} collective-permute-done((f32[2,128,512]{2,1,0:T(8,128)}, f32[2,128,512]{2,1,0:T(8,128)S(1)}, u32[]{:S(2)}, u32[]{:S(2)}) %collective-permute-start.4) | collective-permute-done | bytes 524320 | tf_op jit(solution)/shard_map/ppermute | solution.py:40
  29.1 0.7 fusion.3.win
  29.8 14.7 %waves.1 = (f32[3,256,256]{2,1,0:T(8,128)S(1)}, f32[416,8,128]{2,1,0:T(8,128)S(1)}, f32[416,8,128]{2,1,0:T(8,128)S(1)}) custom-call(s32[1]{0:T(128)} %bitcast.4.column, f32[2,256,256]{2,1,0:T(8,128)S(1)} %fusion.3.win, bf16[2,6,256,256]{3,2,1,0:T(8,128)(2,1)S(1)} %copy-done, f32[256,256]{1,0:T(8,128)S(1)} %bitcast.10, bf16[2,512,512]{2,1,0:T(8,128)(2,1)S(1)} %copy-done.3, ...), custom_call_target="tpu_custom_call" | custom-call | flops 9663676416 | bytes 12582912 | tf_op jit(solution)/shard_map/waves/pallas_call | solution.py:204
  44.5 2.0 collective-permute-start.8
  46.4 3.6 %collective-permute-done.8 = f32[416,8,128]{2,1,0:T(8,128)S(1)} collective-permute-done((f32[416,8,128]{2,1,0:T(8,128)S(1)}, f32[416,8,128]{2,1,0:T(8,128)S(1)}, u32[]{:S(2)}, u32[]{:S(2)}) %collective-permute-start.8) | collective-permute-done | bytes 1703968 | tf_op jit(solution)/shard_map/ppermute | solution.py:272
  50.0 1.4 add.53
  51.3 11.5 %all-to-all-start = ((f32[8,52,8,128]{3,2,1,0:T(8,128)}), f32[8,52,8,128]{3,2,1,0:T(8,128)}, u32[]{:S(2)}, u32[]{:S(2)}) async-start(f32[8,52,8,128]{3,2,1,0:T(8,128)} %bitcast.6), calls=%async_computation | async-start | bytes 3407872 | tf_op jit(solution)/shard_map/all_to_all | solution.py:266
  62.9 0.1 pad_add_fusion.start
  62.9 2.5 place.1
  65.5 1.9 collective-permute-start.5
  67.4 17.7 %all-to-all-done = f32[8,52,8,128]{3,2,1,0:T(8,128)} async-done(((f32[8,52,8,128]{3,2,1,0:T(8,128)}), f32[8,52,8,128]{3,2,1,0:T(8,128)}, u32[]{:S(2)}, u32[]{:S(2)}) %all-to-all-start) | async-done | bytes 1703968 | tf_op jit(solution)/shard_map/all_to_all | solution.py:266
  85.1 1.6 reduce_sum.18
  86.6 0.7 reshape.18
  87.4 44.8 %all-to-all-start.1 = ((f32[16,26,128]{2,1,0:T(8,128)}), f32[16,26,128]{2,1,0:T(8,128)S(1)}, u32[]{:S(2)}, u32[]{:S(2)}) async-start(f32[16,26,128]{2,1,0:T(8,128)} %reshape.18), calls=%async_computation.1 | async-start | bytes 524288 | tf_op jit(solution)/shard_map/all_to_all | solution.py:266
  132.1 1.5 pad_select_fusion
  133.6 0.3 slice_add_fusion.1
  134.0 1.3 collective-permute-start.6
  135.3 4.6 %collective-permute-start.7 = (f32[3,128,512]{2,1,0:T(8,128)S(1)}, f32[3,128,512]{2,1,0:T(8,128)S(1)}, u32[]{:S(2)}, u32[]{:S(2)}) collective-permute-start(f32[3,128,512]{2,1,0:T(8,128)S(1)} %get-tuple-element.17), channel_id=1, source_target_pairs={{0,2},{1,3},{2,4},{3,5},{4,6},{5,7},{6,8},{7,9},{8,10},{9,11},{10,... | collective-permute-start | bytes 2359304 | tf_op jit(solution)/shard_map/ppermute | solution.py:105
  139.9 14.8 %collective-permute-done.6 = f32[3,128,512]{2,1,0:T(8,128)S(1)} collective-permute-done((f32[3,128,512]{2,1,0:T(8,128)S(1)}, f32[3,128,512]{2,1,0:T(8,128)S(1)}, u32[]{:S(2)}, u32[]{:S(2)}) %collective-permute-start.6) | collective-permute-done | bytes 786464 | tf_op jit(solution)/shard_map/ppermute | solution.py:104
  154.8 1.2 collective-permute-done.7
  156.0 0.4 fusion.1
  156.4 0.9 copy-done.5
  157.3 0.7 slice_reduce_fusion
  158.0 4.8 %all-to-all-done.1 = f32[16,26,128]{2,1,0:T(8,128)S(1)} async-done(((f32[16,26,128]{2,1,0:T(8,128)}), f32[16,26,128]{2,1,0:T(8,128)S(1)}, u32[]{:S(2)}, u32[]{:S(2)}) %all-to-all-start.1) | async-done | bytes 213024 | tf_op jit(solution)/shard_map/all_to_all | solution.py:266
  162.8 0.7 concatenate.26
  163.6 63.0 %all_to_all.20 = f32[16,32,128]{2,1,0:T(8,128)S(1)} all-to-all(f32[16,32,128]{2,1,0:T(8,128)S(1)} %broadcast_in_dim.14), channel_id=1, replica_groups=mesh['angle'=2,'row_0'=16,'row_1'=8,'col'=2] {'row_0'}, dimensions={0} | all-to-all | bytes 524288 | tf_op jit(solution)/shard_map/all_to_all | solution.py:266
  226.6 0.6 slice_reduce_fusion.1
  227.2 0.7 concatenate.27
  227.9 0.1 broadcast_in_dim.15
  228.0 29.4 %all_to_all.21.own = f32[8,53,8,128]{3,2,1,0:T(8,128)S(1)} all-to-all(f32[8,53,8,128]{3,2,1,0:T(8,128)S(1)} %broadcast_in_dim.15), channel_id=1, replica_groups=mesh['angle'=2,'row_0'=16,'row_1'=8,'col'=2] {'row_1'}, dimensions={0} | all-to-all | bytes 3473408 | tf_op jit(solution)/shard_map/all_to_all | solution.py:266
  257.5 1.9 collective-permute-start.9
  259.4 0.6 slice_reduce_fusion.3
  260.0 3.0 %collective-permute-done.9.other = f32[8,53,8,128]{3,2,1,0:T(8,128)S(1)} collective-permute-done((f32[8,53,8,128]{3,2,1,0:T(8,128)S(1)}, f32[8,53,8,128]{3,2,1,0:T(8,128)S(1)}, u32[]{:S(2)}, u32[]{:S(2)}) %collective-permute-start.9) | collective-permute-done | bytes 1736736 | tf_op jit(solution)/shard_map/ppermute | solution.py:283
  263.0 0.7 slice_reduce_fusion.2
  265.0 1.1 add_bitcast_fusion
  266.1 2.1 fusion.6
  268.2 2.2 probe_update.1
  (21 shorter events, 0.1 us)
Async XLA Ops:
  0.6 28.5 %copy-start.6 = (f32[2,128,512]{2,1,0:T(8,128)S(1)}, f32[2,128,512]{2,1,0:T(8,128)}, u32[]{:S(2)}) copy-start(f32[2,128,512]{2,1,0:T(8,128)} %param.6) | copy-start | bytes 1572868
  1.7 15.2 %collective-permute-start = (f32[2,128,128]{2,1,0:T(8,128)S(1)}, f32[2,128,128]{2,1,0:T(8,128)S(1)}, u32[]{:S(2)}, u32[]{:S(2)}) collective-permute-start(f32[2,128,128]{2,1,0:T(8,128)S(1)} %slice_select_fusion), channel_id=1, source_target_pairs={{0,3},{1,2},{2,5},{3,4},{4,7},{5,6},{6,9},{7,8},{8,11},{9,10},{10,... | collective-permute-start | bytes 393224 | tf_op jit(solution)/shard_map/ppermute | solution.py:41
  4.8 12.1 %collective-permute-start.1 = (f32[2,128,128]{2,1,0:T(8,128)S(1)}, f32[2,128,128]{2,1,0:T(8,128)S(1)}, u32[]{:S(2)}, u32[]{:S(2)}) collective-permute-start(f32[2,128,128]{2,1,0:T(8,128)S(1)} %slice_select_fusion), channel_id=1, source_target_pairs={{0,1},{1,0},{2,3},{3,2},{4,5},{5,4},{6,7},{7,6},{8,9},{9,8},{10,11... | collective-permute-start | bytes 393224 | tf_op jit(solution)/shard_map/ppermute | solution.py:43
  7.3 9.6 %collective-permute-start.2 = (f32[2,128,128]{2,1,0:T(8,128)S(1)}, f32[2,128,128]{2,1,0:T(8,128)S(1)}, u32[]{:S(2)}, u32[]{:S(2)}) collective-permute-start(f32[2,128,128]{2,1,0:T(8,128)S(1)} %slice_select_fusion), channel_id=1, source_target_pairs={{2,1},{3,0},{4,3},{5,2},{6,5},{7,4},{8,7},{9,6},{10,9},{11,8},{12,... | collective-permute-start | bytes 393224 | tf_op jit(solution)/shard_map/ppermute | solution.py:42
  8.6 16.4 %collective-permute-start.3 = (f32[2,128,512]{2,1,0:T(8,128)}, f32[2,128,512]{2,1,0:T(8,128)S(1)}, u32[]{:S(2)}, u32[]{:S(2)}) collective-permute-start(f32[2,128,512]{2,1,0:T(8,128)} %param.6), channel_id=1, source_target_pairs={{0,2},{1,3},{2,4},{3,5},{4,6},{5,7},{6,8},{7,9},{8,10},{9,11},{10,... | collective-permute-start | bytes 1572872 | tf_op jit(solution)/shard_map/ppermute | solution.py:39
  12.9 16.2 %collective-permute-start.4 = (f32[2,128,512]{2,1,0:T(8,128)}, f32[2,128,512]{2,1,0:T(8,128)S(1)}, u32[]{:S(2)}, u32[]{:S(2)}) collective-permute-start(f32[2,128,512]{2,1,0:T(8,128)} %param.6), channel_id=1, source_target_pairs={{2,0},{3,1},{4,2},{5,3},{6,4},{7,5},{8,6},{9,7},{10,8},{11,9},{12,... | collective-permute-start | bytes 1572872 | tf_op jit(solution)/shard_map/ppermute | solution.py:40
  16.9 12.9 %copy-start = (bf16[2,6,256,256]{3,2,1,0:T(8,128)(2,1)S(1)}, bf16[2,6,256,256]{3,2,1,0:T(8,128)(2,1)}, u32[]{:S(2)}) copy-start(bf16[2,6,256,256]{3,2,1,0:T(8,128)(2,1)} %probe.3) | copy-start | bytes 4718596
  16.9 12.9 %copy-start.2 = (f32[1,256,256]{2,1,0:T(8,128)S(1)}, f32[1,256,256]{2,1,0:T(8,128)}, u32[]{:S(2)}) copy-start(f32[1,256,256]{2,1,0:T(8,128)} %param.9) | copy-start | bytes 786436
  16.9 12.9 %copy-start.3 = (bf16[2,512,512]{2,1,0:T(8,128)(2,1)S(1)}, bf16[2,512,512]{2,1,0:T(8,128)(2,1)}, u32[]{:S(2)}) copy-start(bf16[2,512,512]{2,1,0:T(8,128)(2,1)} %constant.37.clone.forward) | copy-start | bytes 3145732
  16.9 12.9 %copy-start.4 = (bf16[2,512,512]{2,1,0:T(8,128)(2,1)S(1)}, bf16[2,512,512]{2,1,0:T(8,128)(2,1)}, u32[]{:S(2)}) copy-start(bf16[2,512,512]{2,1,0:T(8,128)(2,1)} %constant.38.clone.inverse) | copy-start | bytes 3145732
  44.5 5.5 %collective-permute-start.8 = (f32[416,8,128]{2,1,0:T(8,128)S(1)}, f32[416,8,128]{2,1,0:T(8,128)S(1)}, u32[]{:S(2)}, u32[]{:S(2)}) collective-permute-start(f32[416,8,128]{2,1,0:T(8,128)S(1)} %get-tuple-element.15), channel_id=1, source_target_pairs={{0,1},{1,0},{2,3},{3,2},{4,5},{5,4},{6,7},{7,6},{8,9},{9,8},{10,11... | collective-permute-start | bytes 5111816 | tf_op jit(solution)/shard_map/ppermute | solution.py:272
  51.3 33.7 %all-to-all-start = ((f32[8,52,8,128]{3,2,1,0:T(8,128)}), f32[8,52,8,128]{3,2,1,0:T(8,128)}, u32[]{:S(2)}, u32[]{:S(2)}) async-start(f32[8,52,8,128]{3,2,1,0:T(8,128)} %bitcast.6), calls=%async_computation | async-start | bytes 3407872 | tf_op jit(solution)/shard_map/all_to_all | solution.py:266
  65.5 66.7 %collective-permute-start.5 = (f32[3,384,128]{2,1,0:T(8,128)}, f32[3,384,128]{2,1,0:T(8,128)}, u32[]{:S(2)}, u32[]{:S(2)}) collective-permute-start(f32[3,384,128]{2,1,0:T(8,128)} %get-tuple-element.11), channel_id=1, source_target_pairs={{0,1},{1,0},{2,3},{3,2},{4,5},{5,4},{6,7},{7,6},{8,9},{9,8},{10,11... | collective-permute-start | bytes 1769480 | tf_op jit(solution)/shard_map/ppermute | solution.py:96
  87.4 75.4 %all-to-all-start.1 = ((f32[16,26,128]{2,1,0:T(8,128)}), f32[16,26,128]{2,1,0:T(8,128)S(1)}, u32[]{:S(2)}, u32[]{:S(2)}) async-start(f32[16,26,128]{2,1,0:T(8,128)} %reshape.18), calls=%async_computation.1 | async-start | bytes 524288 | tf_op jit(solution)/shard_map/all_to_all | solution.py:266
  134.0 20.8 %collective-permute-start.6 = (f32[3,128,512]{2,1,0:T(8,128)S(1)}, f32[3,128,512]{2,1,0:T(8,128)S(1)}, u32[]{:S(2)}, u32[]{:S(2)}) collective-permute-start(f32[3,128,512]{2,1,0:T(8,128)S(1)} %get-tuple-element.16), channel_id=1, source_target_pairs={{2,0},{3,1},{4,2},{5,3},{6,4},{7,5},{8,6},{9,7},{10,8},{11,9},{12,... | collective-permute-start | bytes 2359304 | tf_op jit(solution)/shard_map/ppermute | solution.py:104
  135.3 20.7 %collective-permute-start.7 = (f32[3,128,512]{2,1,0:T(8,128)S(1)}, f32[3,128,512]{2,1,0:T(8,128)S(1)}, u32[]{:S(2)}, u32[]{:S(2)}) collective-permute-start(f32[3,128,512]{2,1,0:T(8,128)S(1)} %get-tuple-element.17), channel_id=1, source_target_pairs={{0,2},{1,3},{2,4},{3,5},{4,6},{5,7},{6,8},{7,9},{8,10},{9,11},{10,... | collective-permute-start | bytes 2359304 | tf_op jit(solution)/shard_map/ppermute | solution.py:105
  156.4 0.9 copy-start.5
  257.5 5.6 %collective-permute-start.9 = (f32[8,53,8,128]{3,2,1,0:T(8,128)S(1)}, f32[8,53,8,128]{3,2,1,0:T(8,128)S(1)}, u32[]{:S(2)}, u32[]{:S(2)}) collective-permute-start(f32[8,53,8,128]{3,2,1,0:T(8,128)S(1)} %all_to_all.21.own), channel_id=1, source_target_pairs={{0,1},{1,0},{2,3},{3,2},{4,5},{5,4},{6,7},{7,6},{8,9},{9,8},{10,11... | collective-permute-start | bytes 5210120 | tf_op jit(solution)/shard_map/ppermute | solution.py:283
  265.0 3.2 %copy-start.1 = (bf16[2,6,256,256]{3,2,1,0:T(8,128)(2,1)S(1)}, bf16[2,6,256,256]{3,2,1,0:T(8,128)(2,1)}, u32[]{:S(2)}) copy-start(bf16[2,6,256,256]{3,2,1,0:T(8,128)(2,1)} %probe.3) | copy-start | bytes 4718596

commit v2 on v1

--- a/solution.py
+++ b/solution.py
@@ -49,61 +49,55 @@
     )
 
 
-def place_kernel(start, column, stacked, up, own, down, side, buffer):
-    channels, height, width = stacked.shape
-    rows, cols = own.shape[1:]
+def settle_kernel(starts, column, own, below, above, spot, tile, side, buffer):
+    rows, cols = tile.shape[1:]
+    width = spot.shape[1]
     left_col = column[0] == 0
-    shift = lax.rem(start[1], 128)
-    where = pl.ds(pl.multiple_of(start[1] - shift, 128), width + 128)
     buffer[...] = jnp.zeros_like(buffer)
-
-    @pl.loop(0, channels)
-    def _(k):
-        tall = jnp.concatenate([stacked[k], jnp.zeros((rows, width), jnp.float32)], axis=0)
-        tall = pltpu.roll(tall, start[0], 0)
-        wide = jnp.concatenate([tall, jnp.zeros((height + rows, 128), jnp.float32)], axis=1)
-        buffer[:, where] = pltpu.roll(wide, shift, 1)
-        up[k] = buffer[:rows, rows : rows + cols]
-        own[k] = buffer[rows : 2 * rows, rows : rows + cols]
-        down[k] = buffer[2 * rows :, rows : rows + cols]
-        side[k] = jnp.where(left_col, buffer[:, rows + cols :], buffer[:, :rows])
-
-
-def place(start, column, stacked, rows, cols):
-    channels, height, width = stacked.shape
-    assert height == width == 2 * rows and rows == 128
+    for n, (source, band) in enumerate(((own, 1), (below, 0), (above, 2))):
+        shift = lax.rem(starts[n, 1], 128)
+        where = pl.ds(pl.multiple_of(starts[n, 1] - shift, 128), width + 128)
+        tall = jnp.concatenate([spot[...], jnp.zeros((rows, width), jnp.float32)], axis=0)
+        weight = pltpu.roll(tall, starts[n, 0], 0)[band * rows : (band + 1) * rows]
+        weight = jnp.where(starts[n, 2] == 1, weight, 0.0)
+        for k, piece in enumerate((source[:rows], source[rows : 2 * rows], weight)):
+            wide = jnp.concatenate([piece, jnp.zeros((rows, 128), jnp.float32)], axis=1)
+            buffer[k, :, where] += pltpu.roll(wide, shift, 1)
+    tile[...] = buffer[:, :, rows : rows + cols]
+    side[...] = jnp.where(left_col, buffer[:, :, rows + cols :], buffer[:, :, :rows])
+
+
+def settle(starts, column, own, below, above, spot, rows, cols):
     smem = pl.BlockSpec(memory_space=pltpu.SMEM)
     vmem = pl.BlockSpec(memory_space=pltpu.VMEM)
-    part = jax.ShapeDtypeStruct((channels, rows, cols), jnp.float32)
+    tile = jax.ShapeDtypeStruct((3, rows, cols), jnp.float32)
     return pl.pallas_call(
-        place_kernel,
-        name="place",
-        out_shape=(part, part, part, jax.ShapeDtypeStruct((channels, 3 * rows, rows), jnp.float32)),
-        in_specs=[smem, smem, vmem],
-        out_specs=(vmem,) * 4,
-        scratch_shapes=[pltpu.VMEM((3 * rows, cols + 2 * rows), jnp.float32)],
+        settle_kernel,
+        name="settle",
+        out_shape=(tile, jax.ShapeDtypeStruct((3, rows, rows), jnp.float32)),
+        in_specs=[smem, smem] + [vmem] * 4,
+        out_specs=(vmem, vmem),
+        scratch_shapes=[pltpu.VMEM((3, rows, cols + 2 * rows), jnp.float32)],
         compiler_params=pltpu.CompilerParams(vmem_limit_bytes=24 * 1024 * 1024),
         cost_estimate=pl.CostEstimate(
-            flops=20 * part.size, bytes_accessed=24 * part.size, transcendentals=0
-        ),
-    )(start, column, stacked)
-
-
-def folded_tile(pieces):
-    up, own, down, side = pieces
-    rows, cols = own.shape[1:]
-    left_col = lax.axis_index("col") == 0
+            flops=20 * tile.size, bytes_accessed=12 * tile.size, transcendentals=0
+        ),
+    )(starts, column, own, below, above, spot)
+
+
+def folded_tile(start, column, own, up, down, spot, rows, cols):
+    below = lax.ppermute(up, ROW_COL, partners(-1, False))
+    above = lax.ppermute(down, ROW_COL, partners(1, False))
+    tags = [got[2 * rows, :3].astype(jnp.int32) for got in (below, above)]
+    starts = jnp.stack([jnp.concatenate([start, jnp.ones((1,), jnp.int32)])] + tags)
+    tile, side = settle(starts, column, own, below, above, spot, rows, cols)
     got = lax.ppermute(side, ROW_COL, partners(0, True))
     rest = jnp.zeros(got.shape[:2] + (cols - rows,), got.dtype)
-    got = jnp.where(
-        left_col, jnp.concatenate([rest, got], axis=2), jnp.concatenate([got, rest], axis=2)
-    )
-    up, own, down = (
-        piece + got[:, k * rows : (k + 1) * rows] for k, piece in enumerate((up, own, down))
-    )
-    from_below = lax.ppermute(up, ROW_COL, partners(-1, False))
-    from_above = lax.ppermute(down, ROW_COL, partners(1, False))
-    return own + from_below + from_above
+    return tile + jnp.where(
+        lax.axis_index("col") == 0,
+        jnp.concatenate([rest, got], axis=2),
+        jnp.concatenate([got, rest], axis=2),
+    )
 
 
 def dft_tables(side):
@@ -141,7 +135,9 @@
     )
 
 
-def wave_kernel(column, win, probe, amp, forward, inverse, obj, kept, sent, far, factor):
+def wave_kernel(
+    start, column, win, probe, amp, forward, inverse, own, up, down, spot, kept, sent, far, factor, obj
+):
     modes, side = probe.shape[1], probe.shape[2]
     left_col = column[0] == 0
     tiles = side // 8
@@ -173,6 +169,7 @@
 
     factor[...] = amp[...] / (jnp.sqrt(factor[...]) + 0.5)
     obj[...] = jnp.zeros_like(obj)
+    spot[...] = jnp.zeros_like(spot)
 
     @pl.loop(0, modes)
     def _(m):
@@ -183,7 +180,7 @@
         diff_imag = back[side:] - exit_imag
         obj[0] += probe_real * diff_real + probe_imag * diff_imag
         obj[1] += probe_real * diff_imag - probe_imag * diff_real
-        obj[2] += probe_real * probe_real + probe_imag * probe_imag
+        spot[...] += probe_real * probe_real + probe_imag * probe_imag
         grad_real = win[0] * diff_real + win[1] * diff_imag
         grad_imag = win[0] * diff_imag - win[1] * diff_real
         for half in range(side // 128):
@@ -192,30 +189,43 @@
 
     weight = win[0] * win[0] + win[1] * win[1]
     put(modes * (side // 128) * tiles, weight[:, :128], weight[:, 128:])
-
-
-def waves(column, window, probe, amplitude):
+    rows = side // 2
+    for k in range(2):
+        tall = jnp.concatenate([obj[k], jnp.zeros((rows, side), jnp.float32)], axis=0)
+        tall = pltpu.roll(tall, start[0], 0)
+        for band, out in enumerate((up, own, down)):
+            out[k * rows : (k + 1) * rows] = tall[band * rows : (band + 1) * rows]
+    lane = lax.broadcasted_iota(jnp.int32, (8, side), 1)
+    tag = jnp.where(lane == 0, start[0], jnp.where(lane == 1, start[1], 1)).astype(jnp.float32)
+    up[2 * rows :] = tag
+    down[2 * rows :] = tag
+
+
+def waves(start, column, window, probe, amplitude):
     modes, side = probe.shape[1], probe.shape[2]
     assert side == 256
     forward, inverse = (jnp.asarray(np.stack(table)) for table in dft_tables(side))
     flops = 4 * modes * 2 * side * (6 * side) * (2 * side)
     half = jax.ShapeDtypeStruct(((2 * modes + 1) * (side // 8),) + TILE, jnp.float32)
+    square = jax.ShapeDtypeStruct((side, side), jnp.float32)
+    band = jax.ShapeDtypeStruct((side + 8, side), jnp.float32)
     vmem = pl.BlockSpec(memory_space=pltpu.VMEM)
     return pl.pallas_call(
         wave_kernel,
         name="waves",
-        out_shape=(jax.ShapeDtypeStruct((3, side, side), jnp.float32), half, half),
-        in_specs=[pl.BlockSpec(memory_space=pltpu.SMEM)] + [vmem] * 5,
-        out_specs=(vmem, vmem, vmem),
+        out_shape=(square, band, band, square, half, half),
+        in_specs=[pl.BlockSpec(memory_space=pltpu.SMEM)] * 2 + [vmem] * 5,
+        out_specs=(vmem,) * 6,
         scratch_shapes=[
             pltpu.VMEM((modes, 2 * side, side), jnp.float32),
             pltpu.VMEM((side, side), jnp.float32),
+            pltpu.VMEM((2, side, side), jnp.float32),
         ],
         compiler_params=pltpu.CompilerParams(vmem_limit_bytes=40 * 1024 * 1024),
         cost_estimate=pl.CostEstimate(
             flops=flops, bytes_accessed=12 * 1024 * 1024, transcendentals=0
         ),
-    )(column, window, probe, amplitude, forward, inverse)
+    )(start, column, window, probe, amplitude, forward, inverse)
 
 
 def probe_kernel(column, own, other, probe, out):
@@ -294,9 +304,10 @@
     column = lax.axis_index("col").astype(jnp.int32).reshape(1)
     extended = extended_tile(obj_field, margin)
     window = lax.dynamic_slice(extended, (zero, start_row, start_col), (2, side, side))
-    stacked, kept, sent = waves(column, window, probe_modes, amplitudes[0])
     start = jnp.stack([start_row, start_col])
-    folded = folded_tile(place(start, column, stacked, tile_rows, tile_cols))
+    assert side == 2 * tile_rows == 256
+    own, up, down, spot, kept, sent = waves(start, column, window, probe_modes, amplitudes[0])
+    folded = folded_tile(start, column, own, up, down, spot, tile_rows, tile_cols)
     illumination = folded[2]
     own, other, peak = sum_and_peak(kept, sent, jnp.max(illumination))
     new_object = obj_field + folded[:2] / (illumination + 0.1 * peak)

time: 274 us -> 265 us (0.967)
  blocking collectives: 92.5 us -> 117 us
  starting transfers between devices: 80.5 us -> 66.8 us
  waiting for transfers between devices: 57.2 us -> 43.7 us
  other arithmetic: 12.8 us -> 8.16 us
    all_to_all x2 -> x3, blocking collectives: 92.5 us -> 117 us  [exchange(): return lax.all_to_all(chunks, axis, 0, 0, tiled=True)]
    all_to_all x2 -> x1, starting transfers between devices: 56.3 us -> 44.8 us  [exchange(): return lax.all_to_all(chunks, axis, 0, 0, tiled=True)]
    ppermute x2, waiting for transfers between devices: 16.1 us -> 7 us  [the longest x1 4.16 us: folded_tile(): below = lax.ppermute(up, ROW_COL, partners(-1, False))]
    all_to_all x2 -> x1, waiting for transfers between devices: 22.5 us -> 16.8 us  [exchange(): return lax.all_to_all(chunks, axis, 0, 0, tiled=True)]
  transfers between devices with their start and end apart: 12 -> 11, of which waited for: 8 -> 8; matrix products, arithmetic and copies ran while one was open for 3% -> 1% of each run, Pallas kernels for 1% -> 0%
where the time goes in v2:
time: 265 us; the launch traced here: 263 us
  blocking collectives  117 us (44%)
  starting transfers between devices  66.8 us (25%)
  waiting for transfers between devices  43.7 us (16%)
  Pallas kernels  18.9 us (7%)
  other arithmetic  8.16 us (3%)
  local copies, waits for them, and re-layouts  4.48 us (2%)
  between operations  3.58 us (1%)
    all_to_all x3, blocking collectives, exchange(): return lax.all_to_all(chunks, axis, 0, 0, tiled=True)  117 us
    all_to_all x1, starting transfers between devices, exchange(): return lax.all_to_all(chunks, axis, 0, 0, tiled=True)  44.8 us
    all_to_all x1, waiting for transfers between devices, exchange(): return lax.all_to_all(chunks, axis, 0, 0, tiled=True)  16.8 us
    pallas_call x1, Pallas kernels, waves(): pl.pallas_call(wave_kernel, name='waves', out_shape=(square, band, band,...  15.4 us
    ppermute x1, waiting for transfers between devices, extended_tile(): above = lax.ppermute(block, ROW_COL, partners(1, False))  7.91 us
  transfers between devices with their start and end apart: 11, of which 8 were waited for; matrix products, arithmetic and copies ran while one was open for 1% of the time, Pallas kernels for 0%

profile of v2, /device:TPU:40, one launch (start us, length us, event | category | flops | bytes accessed | tf_op | source)
XLA Modules:
  0.0 263.1 jit_solution(2299348455463625145)
XLA Ops:
  0.6 0.0 copy-start.6
  0.6 1.0 slice_select_fusion
  1.7 3.1 %collective-permute-start = (f32[2,128,128]{2,1,0:T(8,128)S(1)}, f32[2,128,128]{2,1,0:T(8,128)S(1)}, u32[]{:S(2)}, u32[]{:S(2)}) collective-permute-start(f32[2,128,128]{2,1,0:T(8,128)S(1)} %slice_select_fusion), channel_id=1, source_target_pairs={{0,3},{1,2},{2,5},{3,4},{4,7},{5,6},{6,9},{7,8},{8,11},{9,10},{10,... | collective-permute-start | bytes 393224 | tf_op jit(solution)/shard_map/ppermute | solution.py:41
  4.8 2.5 collective-permute-start.1
  7.3 1.3 collective-permute-start.2
  8.6 4.2 %collective-permute-start.3 = (f32[2,128,512]{2,1,0:T(8,128)}, f32[2,128,512]{2,1,0:T(8,128)S(1)}, u32[]{:S(2)}, u32[]{:S(2)}) collective-permute-start(f32[2,128,512]{2,1,0:T(8,128)} %param.6), channel_id=1, source_target_pairs={{0,2},{1,3},{2,4},{3,5},{4,6},{5,7},{6,8},{7,9},{8,10},{9,11},{10,... | collective-permute-start | bytes 1572872 | tf_op jit(solution)/shard_map/ppermute | solution.py:39
  12.9 1.3 collective-permute-start.4
  14.2 1.3 fusion.5
  16.8 0.1 pad_add_fusion.1.start
  17.0 0.0 copy-start.4
  17.0 0.1 broadcast_select_fusion
  17.1 0.0 copy-start.3
  17.1 7.9 %collective-permute-done.3 = f32[2,128,512]{2,1,0:T(8,128)S(1)} collective-permute-done((f32[2,128,512]{2,1,0:T(8,128)}, f32[2,128,512]{2,1,0:T(8,128)S(1)}, u32[]{:S(2)}, u32[]{:S(2)}) %collective-permute-start.3) | collective-permute-done | bytes 524320 | tf_op jit(solution)/shard_map/ppermute | solution.py:39
  25.0 4.1 %collective-permute-done.4 = f32[2,128,512]{2,1,0:T(8,128)S(1)} collective-permute-done((f32[2,128,512]{2,1,0:T(8,128)}, f32[2,128,512]{2,1,0:T(8,128)S(1)}, u32[]{:S(2)}, u32[]{:S(2)}) %collective-permute-start.4) | collective-permute-done | bytes 524320 | tf_op jit(solution)/shard_map/ppermute | solution.py:40
  29.1 0.7 fusion.1.win
  29.8 15.4 %waves.1 = (f32[256,256]{1,0:T(8,128)S(1)}, f32[264,256]{1,0:T(8,128)S(1)}, f32[264,256]{1,0:T(8,128)S(1)}, f32[256,256]{1,0:T(8,128)S(1)}, f32[416,8,128]{2,1,0:T(8,128)S(1)}, /*index=5*/f32[416,8,128]{2,1,0:T(8,128)S(1)}) custom-call(s32[2]{0:T(128)S(1)} %pad_add_fusion.1.start, s32[1]{0:T(128)} %bitcast.5.column, f32[2,256,256]{2,1,0:T(8,128)S(1)} %fusion.1.win, ...), custom_call_target="tpu_custom_call" | custom-call | flops 9663676416 | bytes 12582912 | tf_op jit(solution)/shard_map/waves/pallas_call | solution.py:213
  45.2 2.0 collective-permute-start.8
  47.2 3.6 %collective-permute-done.8 = f32[416,8,128]{2,1,0:T(8,128)S(1)} collective-permute-done((f32[416,8,128]{2,1,0:T(8,128)S(1)}, f32[416,8,128]{2,1,0:T(8,128)S(1)}, u32[]{:S(2)}, u32[]{:S(2)}) %collective-permute-start.8) | collective-permute-done | bytes 1703968 | tf_op jit(solution)/shard_map/ppermute | solution.py:282
  50.7 0.2 add.37
  50.9 34.3 %all_to_all.20 = f32[8,52,8,128]{3,2,1,0:T(8,128)S(1)} all-to-all(f32[8,52,8,128]{3,2,1,0:T(8,128)S(1)} %bitcast.13), channel_id=1, replica_groups=mesh['angle'=2,'row_0'=16,'row_1'=8,'col'=2] {'row_1'}, dimensions={0} | all-to-all | bytes 3407872 | tf_op jit(solution)/shard_map/all_to_all | solution.py:276
  85.2 0.1 reduce_sum.18
  85.3 0.7 reshape.18
  86.1 44.8 %all-to-all-start.1 = ((f32[16,26,128]{2,1,0:T(8,128)}), f32[16,26,128]{2,1,0:T(8,128)S(1)}, u32[]{:S(2)}, u32[]{:S(2)}) async-start(f32[16,26,128]{2,1,0:T(8,128)} %reshape.18), calls=%async_computation.1 | async-start | bytes 524288 | tf_op jit(solution)/shard_map/all_to_all | solution.py:276
  130.8 2.5 collective-permute-start.6
  133.3 1.3 collective-permute-start.5
  134.6 0.1 add_bitcast_fusion.1
  134.7 2.8 %collective-permute-done.6.above = f32[264,256]{1,0:T(8,128)S(1)} collective-permute-done((f32[264,256]{1,0:T(8,128)S(1)}, f32[264,256]{1,0:T(8,128)S(1)}, u32[]{:S(2)}, u32[]{:S(2)}) %collective-permute-start.6) | collective-permute-done | bytes 270368 | tf_op jit(solution)/shard_map/ppermute | solution.py:90
  137.5 4.2 %collective-permute-done.5.below = f32[264,256]{1,0:T(8,128)S(1)} collective-permute-done((f32[264,256]{1,0:T(8,128)S(1)}, f32[264,256]{1,0:T(8,128)S(1)}, u32[]{:S(2)}, u32[]{:S(2)}) %collective-permute-start.5) | collective-permute-done | bytes 270368 | tf_op jit(solution)/shard_map/ppermute | solution.py:89
  141.7 1.2 settle.1
  142.9 2.0 collective-permute-start.7
  144.9 1.4 collective-permute-done.7
  146.3 0.1 select_add_fusion
  146.4 0.9 copy-done.5
  147.3 0.7 slice_reduce_fusion
  148.0 16.8 %all-to-all-done.1 = f32[16,26,128]{2,1,0:T(8,128)S(1)} async-done(((f32[16,26,128]{2,1,0:T(8,128)}), f32[16,26,128]{2,1,0:T(8,128)S(1)}, u32[]{:S(2)}, u32[]{:S(2)}) %all-to-all-start.1) | async-done | bytes 213024 | tf_op jit(solution)/shard_map/all_to_all | solution.py:276
  164.8 0.7 concatenate.31
  165.6 52.6 %all_to_all.21 = f32[16,32,128]{2,1,0:T(8,128)S(1)} all-to-all(f32[16,32,128]{2,1,0:T(8,128)S(1)} %broadcast_in_dim.14), channel_id=1, replica_groups=mesh['angle'=2,'row_0'=16,'row_1'=8,'col'=2] {'row_0'}, dimensions={0} | all-to-all | bytes 524288 | tf_op jit(solution)/shard_map/all_to_all | solution.py:276
  218.2 0.6 slice_reduce_fusion.1
  218.8 0.7 concatenate.32
  219.5 0.1 broadcast_in_dim.15
  219.6 30.4 %all_to_all.22.own = f32[8,53,8,128]{3,2,1,0:T(8,128)S(1)} all-to-all(f32[8,53,8,128]{3,2,1,0:T(8,128)S(1)} %broadcast_in_dim.15), channel_id=1, replica_groups=mesh['angle'=2,'row_0'=16,'row_1'=8,'col'=2] {'row_1'}, dimensions={0} | all-to-all | bytes 3473408 | tf_op jit(solution)/shard_map/all_to_all | solution.py:276
  250.0 1.9 collective-permute-start.9
  252.0 0.6 slice_reduce_fusion.3
  252.6 3.0 %collective-permute-done.9.other = f32[8,53,8,128]{3,2,1,0:T(8,128)S(1)} collective-permute-done((f32[8,53,8,128]{3,2,1,0:T(8,128)S(1)}, f32[8,53,8,128]{3,2,1,0:T(8,128)S(1)}, u32[]{:S(2)}, u32[]{:S(2)}) %collective-permute-start.9) | collective-permute-done | bytes 1736736 | tf_op jit(solution)/shard_map/ppermute | solution.py:293
  255.6 0.7 slice_reduce_fusion.2
  257.6 1.1 add_bitcast_fusion
  258.7 2.1 fusion.4
  260.8 2.2 probe_update.1
  (22 shorter events, 0.2 us)
Async XLA Ops:
  0.6 28.5 %copy-start.6 = (f32[2,128,512]{2,1,0:T(8,128)S(1)}, f32[2,128,512]{2,1,0:T(8,128)}, u32[]{:S(2)}) copy-start(f32[2,128,512]{2,1,0:T(8,128)} %param.6) | copy-start | bytes 1572868
  1.7 15.2 %collective-permute-start = (f32[2,128,128]{2,1,0:T(8,128)S(1)}, f32[2,128,128]{2,1,0:T(8,128)S(1)}, u32[]{:S(2)}, u32[]{:S(2)}) collective-permute-start(f32[2,128,128]{2,1,0:T(8,128)S(1)} %slice_select_fusion), channel_id=1, source_target_pairs={{0,3},{1,2},{2,5},{3,4},{4,7},{5,6},{6,9},{7,8},{8,11},{9,10},{10,... | collective-permute-start | bytes 393224 | tf_op jit(solution)/shard_map/ppermute | solution.py:41
  4.8 12.2 %collective-permute-start.1 = (f32[2,128,128]{2,1,0:T(8,128)S(1)}, f32[2,128,128]{2,1,0:T(8,128)S(1)}, u32[]{:S(2)}, u32[]{:S(2)}) collective-permute-start(f32[2,128,128]{2,1,0:T(8,128)S(1)} %slice_select_fusion), channel_id=1, source_target_pairs={{0,1},{1,0},{2,3},{3,2},{4,5},{5,4},{6,7},{7,6},{8,9},{9,8},{10,11... | collective-permute-start | bytes 393224 | tf_op jit(solution)/shard_map/ppermute | solution.py:43
  7.3 9.6 %collective-permute-start.2 = (f32[2,128,128]{2,1,0:T(8,128)S(1)}, f32[2,128,128]{2,1,0:T(8,128)S(1)}, u32[]{:S(2)}, u32[]{:S(2)}) collective-permute-start(f32[2,128,128]{2,1,0:T(8,128)S(1)} %slice_select_fusion), channel_id=1, source_target_pairs={{2,1},{3,0},{4,3},{5,2},{6,5},{7,4},{8,7},{9,6},{10,9},{11,8},{12,... | collective-permute-start | bytes 393224 | tf_op jit(solution)/shard_map/ppermute | solution.py:42
  8.6 16.4 %collective-permute-start.3 = (f32[2,128,512]{2,1,0:T(8,128)}, f32[2,128,512]{2,1,0:T(8,128)S(1)}, u32[]{:S(2)}, u32[]{:S(2)}) collective-permute-start(f32[2,128,512]{2,1,0:T(8,128)} %param.6), channel_id=1, source_target_pairs={{0,2},{1,3},{2,4},{3,5},{4,6},{5,7},{6,8},{7,9},{8,10},{9,11},{10,... | collective-permute-start | bytes 1572872 | tf_op jit(solution)/shard_map/ppermute | solution.py:39
  12.9 16.2 %collective-permute-start.4 = (f32[2,128,512]{2,1,0:T(8,128)}, f32[2,128,512]{2,1,0:T(8,128)S(1)}, u32[]{:S(2)}, u32[]{:S(2)}) collective-permute-start(f32[2,128,512]{2,1,0:T(8,128)} %param.6), channel_id=1, source_target_pairs={{2,0},{3,1},{4,2},{5,3},{6,4},{7,5},{8,6},{9,7},{10,8},{11,9},{12,... | collective-permute-start | bytes 1572872 | tf_op jit(solution)/shard_map/ppermute | solution.py:40
  17.0 12.8 %copy-start.4 = (bf16[2,512,512]{2,1,0:T(8,128)(2,1)S(1)}, bf16[2,512,512]{2,1,0:T(8,128)(2,1)}, u32[]{:S(2)}) copy-start(bf16[2,512,512]{2,1,0:T(8,128)(2,1)} %constant.40.clone.inverse) | copy-start | bytes 3145732
  17.1 12.7 %copy-start = (bf16[2,6,256,256]{3,2,1,0:T(8,128)(2,1)S(1)}, bf16[2,6,256,256]{3,2,1,0:T(8,128)(2,1)}, u32[]{:S(2)}) copy-start(bf16[2,6,256,256]{3,2,1,0:T(8,128)(2,1)} %probe.3) | copy-start | bytes 4718596
  17.1 12.7 %copy-start.2 = (f32[1,256,256]{2,1,0:T(8,128)S(1)}, f32[1,256,256]{2,1,0:T(8,128)}, u32[]{:S(2)}) copy-start(f32[1,256,256]{2,1,0:T(8,128)} %param.9) | copy-start | bytes 786436
  17.1 12.7 %copy-start.3 = (bf16[2,512,512]{2,1,0:T(8,128)(2,1)S(1)}, bf16[2,512,512]{2,1,0:T(8,128)(2,1)}, u32[]{:S(2)}) copy-start(bf16[2,512,512]{2,1,0:T(8,128)(2,1)} %constant.39.clone.forward) | copy-start | bytes 3145732
  45.2 5.5 %collective-permute-start.8 = (f32[416,8,128]{2,1,0:T(8,128)S(1)}, f32[416,8,128]{2,1,0:T(8,128)S(1)}, u32[]{:S(2)}, u32[]{:S(2)}) collective-permute-start(f32[416,8,128]{2,1,0:T(8,128)S(1)} %get-tuple-element.17), channel_id=1, source_target_pairs={{0,1},{1,0},{2,3},{3,2},{4,5},{5,4},{6,7},{7,6},{8,9},{9,8},{10,11... | collective-permute-start | bytes 5111816 | tf_op jit(solution)/shard_map/ppermute | solution.py:282
  86.1 78.8 %all-to-all-start.1 = ((f32[16,26,128]{2,1,0:T(8,128)}), f32[16,26,128]{2,1,0:T(8,128)S(1)}, u32[]{:S(2)}, u32[]{:S(2)}) async-start(f32[16,26,128]{2,1,0:T(8,128)} %reshape.18), calls=%async_computation.1 | async-start | bytes 524288 | tf_op jit(solution)/shard_map/all_to_all | solution.py:276
  130.8 6.7 %collective-permute-start.6 = (f32[264,256]{1,0:T(8,128)S(1)}, f32[264,256]{1,0:T(8,128)S(1)}, u32[]{:S(2)}, u32[]{:S(2)}) collective-permute-start(f32[264,256]{1,0:T(8,128)S(1)} %get-tuple-element.11), channel_id=1, source_target_pairs={{0,2},{1,3},{2,4},{3,5},{4,6},{5,7},{6,8},{7,9},{8,10},{9,11},{10,... | collective-permute-start | bytes 811016 | tf_op jit(solution)/shard_map/ppermute | solution.py:90
  133.3 8.4 %collective-permute-start.5 = (f32[264,256]{1,0:T(8,128)S(1)}, f32[264,256]{1,0:T(8,128)S(1)}, u32[]{:S(2)}, u32[]{:S(2)}) collective-permute-start(f32[264,256]{1,0:T(8,128)S(1)} %get-tuple-element.10), channel_id=1, source_target_pairs={{2,0},{3,1},{4,2},{5,3},{6,4},{7,5},{8,6},{9,7},{10,8},{11,9},{12,... | collective-permute-start | bytes 811016 | tf_op jit(solution)/shard_map/ppermute | solution.py:89
  142.9 3.4 %collective-permute-start.7 = (f32[3,128,128]{2,1,0:T(8,128)S(1)}, f32[3,128,128]{2,1,0:T(8,128)S(1)}, u32[]{:S(2)}, u32[]{:S(2)}) collective-permute-start(f32[3,128,128]{2,1,0:T(8,128)S(1)} %get-tuple-element.15), channel_id=1, source_target_pairs={{0,1},{1,0},{2,3},{3,2},{4,5},{5,4},{6,7},{7,6},{8,9},{9,8},{10,11... | collective-permute-start | bytes 589832 | tf_op jit(solution)/shard_map/ppermute | solution.py:94
  146.4 0.9 copy-start.5
  250.0 5.6 %collective-permute-start.9 = (f32[8,53,8,128]{3,2,1,0:T(8,128)S(1)}, f32[8,53,8,128]{3,2,1,0:T(8,128)S(1)}, u32[]{:S(2)}, u32[]{:S(2)}) collective-permute-start(f32[8,53,8,128]{3,2,1,0:T(8,128)S(1)} %all_to_all.22.own), channel_id=1, source_target_pairs={{0,1},{1,0},{2,3},{3,2},{4,5},{5,4},{6,7},{7,6},{8,9},{9,8},{10,11... | collective-permute-start | bytes 5210120 | tf_op jit(solution)/shard_map/ppermute | solution.py:293
  257.6 3.2 %copy-start.1 = (bf16[2,6,256,256]{3,2,1,0:T(8,128)(2,1)S(1)}, bf16[2,6,256,256]{3,2,1,0:T(8,128)(2,1)}, u32[]{:S(2)}) copy-start(bf16[2,6,256,256]{3,2,1,0:T(8,128)(2,1)} %probe.3) | copy-start | bytes 4718596

commit v3 on v2

--- a/solution.py
+++ b/solution.py
@@ -11,11 +11,11 @@
 from jax.sharding import PartitionSpec as P
 
 
-ROW = ("row_0", "row_1")
+ROW = ("row_0", "row_1", "row_2")
 ROW_COL = ROW + ("col",)
 ANGLE_ROW = ("angle",) + ROW
 ANGLE_ROW_COL = ANGLE_ROW + ("col",)
-NEAR = 8
+NEAR, MIDDLE = 4, 4
 TILE = (8, 128)
 
 
@@ -277,21 +277,30 @@
 
 
 def sum_and_peak(kept, sent, local_peak):
-    far, near = (lax.axis_size(axis) for axis in ROW)
     swap = [(0, 1), (1, 0)]
     tiles = kept + lax.ppermute(sent, "col", swap)
-    tiles = tiles.reshape((near, tiles.shape[0] // near) + TILE)
-    tiles = jnp.sum(exchange(tiles, "row_1"), axis=0)
+    for axis in ROW[:0:-1]:
+        count = lax.axis_size(axis)
+        tiles = tiles.reshape((count, tiles.shape[0] // count) + TILE)
+        tiles = jnp.sum(exchange(tiles, axis), axis=0)
+    far = lax.axis_size(ROW[0])
     part = tiles.shape[0] * TILE[0] // far
-    rows = jnp.sum(exchange(tiles.reshape(far, part, 128), "row_0"), axis=0)
+    rows = jnp.sum(exchange(tiles.reshape(far, part, 128), ROW[0]), axis=0)
+    seen = lax.ppermute(jnp.full(TILE, local_peak), "col", swap)
+    local_peak = jnp.maximum(local_peak, jnp.max(seen))
     spare = jnp.full((TILE[0] - part % TILE[0], 128), local_peak)
     rows = jnp.concatenate([rows, spare])
-    got = exchange(jnp.broadcast_to(rows, (far,) + rows.shape), "row_0")
-    peak = jnp.full((1,) + TILE, jnp.max(got[:, part:]))
-    tiles = jnp.concatenate([got[:, :part].reshape(tiles.shape), peak])
-    own = exchange(jnp.broadcast_to(tiles, (near,) + tiles.shape), "row_1")
+    got = exchange(jnp.broadcast_to(rows, (far,) + rows.shape), ROW[0])
+    peak = jnp.max(got[:, part:])
+    tiles = got[:, :part].reshape(tiles.shape)
+    for axis in ROW[1:]:
+        tiles = jnp.concatenate([tiles, jnp.full((1,) + TILE, peak)])
+        tiles = jnp.broadcast_to(tiles, (lax.axis_size(axis),) + tiles.shape)
+        own = exchange(tiles, axis)
+        peak = jnp.max(own[:, -1])
+        tiles = own[:, :-1].reshape((-1,) + TILE)
     other = lax.ppermute(own, "col", swap)
-    return own, other, jnp.maximum(jnp.max(own[:, -1]), jnp.max(other[:, -1]))
+    return own, other, peak
 
 
 def update(obj_field, probe_modes, centers, amplitudes):
@@ -317,7 +326,11 @@
 def solution(mesh):
     split_mesh = Mesh(
         mesh.devices.reshape(
-            mesh.shape["angle"], mesh.shape["row"] // NEAR, NEAR, mesh.shape["col"]
+            mesh.shape["angle"],
+            mesh.shape["row"] // (NEAR * MIDDLE),
+            MIDDLE,
+            NEAR,
+            mesh.shape["col"],
         ),
         ANGLE_ROW_COL,
     )

time: 265 us -> 263 us (level)
  blocking collectives: 117 us -> 106 us
  starting transfers between devices: 66.8 us -> 77.5 us
  waiting for transfers between devices: 43.7 us -> 39.7 us
    all_to_all x3 -> x4, blocking collectives: 117 us -> 106 us  [exchange(): return lax.all_to_all(chunks, axis, 0, 0, tiled=True)]
    all_to_all x1 -> x2, starting transfers between devices: 44.8 us -> 51.2 us  [exchange(): return lax.all_to_all(chunks, axis, 0, 0, tiled=True)]
    ppermute x1, waiting for transfers between devices: 3 us -> 0.01 us  [sum_and_peak(): other = lax.ppermute(own, 'col', swap)]
    ppermute x1, waiting for transfers between devices: 2.84 us -> 0.01 us  [folded_tile(): above = lax.ppermute(down, ROW_COL, partners(1, False))]
    all_to_all x1 -> x2, waiting for transfers between devices: 16.8 us -> 19 us  [exchange(): return lax.all_to_all(chunks, axis, 0, 0, tiled=True)]
  transfers between devices with their start and end apart: 11 -> 13, of which waited for: 8 -> 8; matrix products, arithmetic and copies ran while one was open for 1% -> 3% of each run, Pallas kernels for 0% -> 0%
where the time goes in v3:
time: 263 us; the launch traced here: 261 us
  blocking collectives  106 us (40%)
  starting transfers between devices  77.5 us (29%)
  waiting for transfers between devices  39.7 us (15%)
  Pallas kernels  19 us (7%)
  other arithmetic  9.42 us (4%)
  local copies, waits for them, and re-layouts  5.06 us (2%)
  between operations  4.17 us (2%)
    all_to_all x4, blocking collectives, exchange(): return lax.all_to_all(chunks, axis, 0, 0, tiled=True)  106 us
    all_to_all x2, starting transfers between devices, exchange(): return lax.all_to_all(chunks, axis, 0, 0, tiled=True)  51.2 us
    all_to_all x2, waiting for transfers between devices, exchange(): return lax.all_to_all(chunks, axis, 0, 0, tiled=True)  19 us
    pallas_call x1, Pallas kernels, waves(): pl.pallas_call(wave_kernel, name='waves', out_shape=(square, band, band,...  15.5 us
    ppermute x1, waiting for transfers between devices, extended_tile(): above = lax.ppermute(block, ROW_COL, partners(1, False))  7.92 us
  transfers between devices with their start and end apart: 13, of which 8 were waited for; matrix products, arithmetic and copies ran while one was open for 3% of the time, Pallas kernels for 0%

profile of v3, /device:TPU:40, one launch (start us, length us, event | category | flops | bytes accessed | tf_op | source)
XLA Modules:
  0.0 260.6 jit_solution(15304988620084214999)
XLA Ops:
  0.6 1.0 slice_select_fusion
  1.7 1.3 collective-permute-start.2
  3.0 2.0 collective-permute-start.1
  5.0 4.3 %collective-permute-start = (f32[2,128,128]{2,1,0:T(8,128)S(1)}, f32[2,128,128]{2,1,0:T(8,128)S(1)}, u32[]{:S(2)}, u32[]{:S(2)}) collective-permute-start(f32[2,128,128]{2,1,0:T(8,128)S(1)} %slice_select_fusion), channel_id=1, source_target_pairs={{0,3},{1,2},{2,5},{3,4},{4,7},{5,6},{6,9},{7,8},{8,11},{9,10},{10,... | collective-permute-start | bytes 393224 | tf_op jit(solution)/shard_map/ppermute | solution.py:41
  9.3 3.6 %collective-permute-start.3 = (f32[2,128,512]{2,1,0:T(8,128)}, f32[2,128,512]{2,1,0:T(8,128)S(1)}, u32[]{:S(2)}, u32[]{:S(2)}) collective-permute-start(f32[2,128,512]{2,1,0:T(8,128)} %param.6), channel_id=1, source_target_pairs={{0,2},{1,3},{2,4},{3,5},{4,6},{5,7},{6,8},{7,9},{8,10},{9,11},{10,... | collective-permute-start | bytes 1572872 | tf_op jit(solution)/shard_map/ppermute | solution.py:39
  12.9 1.3 collective-permute-start.4
  14.2 1.3 fusion.5
  17.1 7.9 %collective-permute-done.3 = f32[2,128,512]{2,1,0:T(8,128)S(1)} collective-permute-done((f32[2,128,512]{2,1,0:T(8,128)}, f32[2,128,512]{2,1,0:T(8,128)S(1)}, u32[]{:S(2)}, u32[]{:S(2)}) %collective-permute-start.3) | collective-permute-done | bytes 524320 | tf_op jit(solution)/shard_map/ppermute | solution.py:39
  25.0 4.1 %collective-permute-done.4 = f32[2,128,512]{2,1,0:T(8,128)S(1)} collective-permute-done((f32[2,128,512]{2,1,0:T(8,128)}, f32[2,128,512]{2,1,0:T(8,128)S(1)}, u32[]{:S(2)}, u32[]{:S(2)}) %collective-permute-start.4) | collective-permute-done | bytes 524320 | tf_op jit(solution)/shard_map/ppermute | solution.py:40
  29.1 0.7 fusion.1.win
  29.8 15.5 %waves.1 = (f32[256,256]{1,0:T(8,128)S(1)}, f32[264,256]{1,0:T(8,128)S(1)}, f32[264,256]{1,0:T(8,128)S(1)}, f32[256,256]{1,0:T(8,128)S(1)}, f32[416,8,128]{2,1,0:T(8,128)S(1)}, /*index=5*/f32[416,8,128]{2,1,0:T(8,128)S(1)}) custom-call(s32[2]{0:T(128)S(1)} %pad_add_fusion.1.start, s32[1]{0:T(128)} %bitcast.5.column, f32[2,256,256]{2,1,0:T(8,128)S(1)} %fusion.1.win, ...), custom_call_target="tpu_custom_call" | custom-call | flops 9663676416 | bytes 12582912 | tf_op jit(solution)/shard_map/waves/pallas_call | solution.py:213
  45.3 2.0 collective-permute-start.8
  47.2 3.6 %collective-permute-done.8 = f32[416,8,128]{2,1,0:T(8,128)S(1)} collective-permute-done((f32[416,8,128]{2,1,0:T(8,128)S(1)}, f32[416,8,128]{2,1,0:T(8,128)S(1)}, u32[]{:S(2)}, u32[]{:S(2)}) %collective-permute-start.8) | collective-permute-done | bytes 1703968 | tf_op jit(solution)/shard_map/ppermute | solution.py:281
  50.8 0.2 add.43
  51.0 29.5 %all_to_all.30 = f32[4,104,8,128]{3,2,1,0:T(8,128)S(1)} all-to-all(f32[4,104,8,128]{3,2,1,0:T(8,128)S(1)} %bitcast.15), channel_id=1, replica_groups=mesh['angle'=2,'row_0'=8,'row_1'=4,'row_2'=4,'col'=2] {'row_2'}, dimensions={0} | all-to-all | bytes 3407872 | tf_op jit(solution)/shard_map/all_to_all | solution.py:276
  80.4 0.9 reduce_sum.27
  81.3 10.9 %all-to-all-start.1 = ((f32[4,26,8,128]{3,2,1,0:T(8,128)}), f32[4,26,8,128]{3,2,1,0:T(8,128)S(1)}, u32[]{:S(2)}, u32[]{:S(2)}) async-start(f32[4,26,8,128]{3,2,1,0:T(8,128)} %bitcast.8), calls=%async_computation.1 | async-start | bytes 851968 | tf_op jit(solution)/shard_map/all_to_all | solution.py:276
  92.2 1.3 collective-permute-start.5
  93.5 4.6 %collective-permute-start.6 = (f32[264,256]{1,0:T(8,128)S(1)}, f32[264,256]{1,0:T(8,128)S(1)}, u32[]{:S(2)}, u32[]{:S(2)}) collective-permute-start(f32[264,256]{1,0:T(8,128)S(1)} %get-tuple-element.11), channel_id=1, source_target_pairs={{0,2},{1,3},{2,4},{3,5},{4,6},{5,7},{6,8},{7,9},{8,10},{9,11},{10,... | collective-permute-start | bytes 811016 | tf_op jit(solution)/shard_map/ppermute | solution.py:90
  98.2 0.1 add_bitcast_fusion.1
  98.2 2.7 %collective-permute-done.5.below = f32[264,256]{1,0:T(8,128)S(1)} collective-permute-done((f32[264,256]{1,0:T(8,128)S(1)}, f32[264,256]{1,0:T(8,128)S(1)}, u32[]{:S(2)}, u32[]{:S(2)}) %collective-permute-start.5) | collective-permute-done | bytes 270368 | tf_op jit(solution)/shard_map/ppermute | solution.py:89
  101.0 3.9 %all-to-all-done.1 = f32[4,26,8,128]{3,2,1,0:T(8,128)S(1)} async-done(((f32[4,26,8,128]{3,2,1,0:T(8,128)}), f32[4,26,8,128]{3,2,1,0:T(8,128)S(1)}, u32[]{:S(2)}, u32[]{:S(2)}) %all-to-all-start.1) | async-done | bytes 426016 | tf_op jit(solution)/shard_map/all_to_all | solution.py:276
  104.9 0.7 reshape.25
  105.6 40.3 %all-to-all-start.2 = ((f32[8,26,128]{2,1,0:T(8,128)}), f32[8,26,128]{2,1,0:T(8,128)S(1)}, u32[]{:S(2)}, u32[]{:S(2)}) async-start(f32[8,26,128]{2,1,0:T(8,128)} %reshape.25), calls=%async_computation.2 | async-start | bytes 262144 | tf_op jit(solution)/shard_map/all_to_all | solution.py:276
  145.9 1.3 settle.1
  147.2 2.0 collective-permute-start.7
  149.1 1.4 collective-permute-done.7
  150.5 0.1 select_add_fusion
  150.6 0.9 copy-done.5
  151.5 0.7 slice_reduce_fusion
  152.2 0.6 broadcast_in_dim.21
  152.8 2.1 collective-permute-start.9
  154.9 1.0 collective-permute-done.9
  155.9 0.6 reduce_max.46
  157.7 15.1 %all-to-all-done.2 = f32[8,26,128]{2,1,0:T(8,128)S(1)} async-done(((f32[8,26,128]{2,1,0:T(8,128)}), f32[8,26,128]{2,1,0:T(8,128)S(1)}, u32[]{:S(2)}, u32[]{:S(2)}) %all-to-all-start.2) | async-done | bytes 106528 | tf_op jit(solution)/shard_map/all_to_all | solution.py:276
  172.9 37.3 %all_to_all.31 = f32[8,32,128]{2,1,0:T(8,128)S(1)} all-to-all(f32[8,32,128]{2,1,0:T(8,128)S(1)} %broadcast_in_dim.22), channel_id=1, replica_groups=mesh['angle'=2,'row_0'=8,'row_1'=4,'row_2'=4,'col'=2] {'row_0'}, dimensions={0} | all-to-all | bytes 262144 | tf_op jit(solution)/shard_map/all_to_all | solution.py:276
  210.2 0.6 slice_reduce_fusion.1
  210.8 0.7 concatenate.35
  211.5 14.9 %all_to_all.32 = f32[4,27,8,128]{3,2,1,0:T(8,128)S(1)} all-to-all(f32[4,27,8,128]{3,2,1,0:T(8,128)S(1)} %broadcast_in_dim.23), channel_id=1, replica_groups=mesh['angle'=2,'row_0'=8,'row_1'=4,'row_2'=4,'col'=2] {'row_1'}, dimensions={0} | all-to-all | bytes 884736 | tf_op jit(solution)/shard_map/all_to_all | solution.py:276
  226.4 0.6 slice_reduce_fusion.3
  227.0 0.7 concatenate.36
  227.7 0.1 broadcast_in_dim.24
  227.8 24.1 %all_to_all.33.own = f32[4,105,8,128]{3,2,1,0:T(8,128)S(1)} all-to-all(f32[4,105,8,128]{3,2,1,0:T(8,128)S(1)} %broadcast_in_dim.24), channel_id=1, replica_groups=mesh['angle'=2,'row_0'=8,'row_1'=4,'row_2'=4,'col'=2] {'row_2'}, dimensions={0} | all-to-all | bytes 3440640 | tf_op jit(solution)/shard_map/all_to_all | solution.py:276
  251.9 1.9 collective-permute-start.10
  253.8 0.6 slice_reduce_fusion.2
  255.1 1.1 add_bitcast_fusion
  256.2 2.1 fusion.4
  258.3 2.2 probe_update.1
  (33 shorter events, 0.4 us)
Async XLA Ops:
  0.6 28.5 %copy-start.6 = (f32[2,128,512]{2,1,0:T(8,128)S(1)}, f32[2,128,512]{2,1,0:T(8,128)}, u32[]{:S(2)}) copy-start(f32[2,128,512]{2,1,0:T(8,128)} %param.6) | copy-start | bytes 1572868
  1.7 15.3 %collective-permute-start.2 = (f32[2,128,128]{2,1,0:T(8,128)S(1)}, f32[2,128,128]{2,1,0:T(8,128)S(1)}, u32[]{:S(2)}, u32[]{:S(2)}) collective-permute-start(f32[2,128,128]{2,1,0:T(8,128)S(1)} %slice_select_fusion), channel_id=1, source_target_pairs={{2,1},{3,0},{4,3},{5,2},{6,5},{7,4},{8,7},{9,6},{10,9},{11,8},{12,... | collective-permute-start | bytes 393224 | tf_op jit(solution)/shard_map/ppermute | solution.py:42
  3.0 13.9 %collective-permute-start.1 = (f32[2,128,128]{2,1,0:T(8,128)S(1)}, f32[2,128,128]{2,1,0:T(8,128)S(1)}, u32[]{:S(2)}, u32[]{:S(2)}) collective-permute-start(f32[2,128,128]{2,1,0:T(8,128)S(1)} %slice_select_fusion), channel_id=1, source_target_pairs={{0,1},{1,0},{2,3},{3,2},{4,5},{5,4},{6,7},{7,6},{8,9},{9,8},{10,11... | collective-permute-start | bytes 393224 | tf_op jit(solution)/shard_map/ppermute | solution.py:43
  5.0 11.9 %collective-permute-start = (f32[2,128,128]{2,1,0:T(8,128)S(1)}, f32[2,128,128]{2,1,0:T(8,128)S(1)}, u32[]{:S(2)}, u32[]{:S(2)}) collective-permute-start(f32[2,128,128]{2,1,0:T(8,128)S(1)} %slice_select_fusion), channel_id=1, source_target_pairs={{0,3},{1,2},{2,5},{3,4},{4,7},{5,6},{6,9},{7,8},{8,11},{9,10},{10,... | collective-permute-start | bytes 393224 | tf_op jit(solution)/shard_map/ppermute | solution.py:41
  9.3 15.7 %collective-permute-start.3 = (f32[2,128,512]{2,1,0:T(8,128)}, f32[2,128,512]{2,1,0:T(8,128)S(1)}, u32[]{:S(2)}, u32[]{:S(2)}) collective-permute-start(f32[2,128,512]{2,1,0:T(8,128)} %param.6), channel_id=1, source_target_pairs={{0,2},{1,3},{2,4},{3,5},{4,6},{5,7},{6,8},{7,9},{8,10},{9,11},{10,... | collective-permute-start | bytes 1572872 | tf_op jit(solution)/shard_map/ppermute | solution.py:39
  12.9 16.2 %collective-permute-start.4 = (f32[2,128,512]{2,1,0:T(8,128)}, f32[2,128,512]{2,1,0:T(8,128)S(1)}, u32[]{:S(2)}, u32[]{:S(2)}) collective-permute-start(f32[2,128,512]{2,1,0:T(8,128)} %param.6), channel_id=1, source_target_pairs={{2,0},{3,1},{4,2},{5,3},{6,4},{7,5},{8,6},{9,7},{10,8},{11,9},{12,... | collective-permute-start | bytes 1572872 | tf_op jit(solution)/shard_map/ppermute | solution.py:40
  17.0 12.8 %copy-start.4 = (bf16[2,512,512]{2,1,0:T(8,128)(2,1)S(1)}, bf16[2,512,512]{2,1,0:T(8,128)(2,1)}, u32[]{:S(2)}) copy-start(bf16[2,512,512]{2,1,0:T(8,128)(2,1)} %constant.44.clone.forward) | copy-start | bytes 3145732
  17.1 12.7 %copy-start = (bf16[2,6,256,256]{3,2,1,0:T(8,128)(2,1)S(1)}, bf16[2,6,256,256]{3,2,1,0:T(8,128)(2,1)}, u32[]{:S(2)}) copy-start(bf16[2,6,256,256]{3,2,1,0:T(8,128)(2,1)} %probe.3) | copy-start | bytes 4718596
  17.1 12.7 %copy-start.2 = (f32[1,256,256]{2,1,0:T(8,128)S(1)}, f32[1,256,256]{2,1,0:T(8,128)}, u32[]{:S(2)}) copy-start(f32[1,256,256]{2,1,0:T(8,128)} %param.9) | copy-start | bytes 786436
  17.1 12.7 %copy-start.3 = (bf16[2,512,512]{2,1,0:T(8,128)(2,1)S(1)}, bf16[2,512,512]{2,1,0:T(8,128)(2,1)}, u32[]{:S(2)}) copy-start(bf16[2,512,512]{2,1,0:T(8,128)(2,1)} %constant.45.clone.inverse) | copy-start | bytes 3145732
  45.3 5.5 %collective-permute-start.8 = (f32[416,8,128]{2,1,0:T(8,128)S(1)}, f32[416,8,128]{2,1,0:T(8,128)S(1)}, u32[]{:S(2)}, u32[]{:S(2)}) collective-permute-start(f32[416,8,128]{2,1,0:T(8,128)S(1)} %get-tuple-element.17), channel_id=1, source_target_pairs={{0,1},{1,0},{2,3},{3,2},{4,5},{5,4},{6,7},{7,6},{8,9},{9,8},{10,11... | collective-permute-start | bytes 5111816 | tf_op jit(solution)/shard_map/ppermute | solution.py:281
  81.3 23.6 %all-to-all-start.1 = ((f32[4,26,8,128]{3,2,1,0:T(8,128)}), f32[4,26,8,128]{3,2,1,0:T(8,128)S(1)}, u32[]{:S(2)}, u32[]{:S(2)}) async-start(f32[4,26,8,128]{3,2,1,0:T(8,128)} %bitcast.8), calls=%async_computation.1 | async-start | bytes 851968 | tf_op jit(solution)/shard_map/all_to_all | solution.py:276
  92.2 8.7 %collective-permute-start.5 = (f32[264,256]{1,0:T(8,128)S(1)}, f32[264,256]{1,0:T(8,128)S(1)}, u32[]{:S(2)}, u32[]{:S(2)}) collective-permute-start(f32[264,256]{1,0:T(8,128)S(1)} %get-tuple-element.10), channel_id=1, source_target_pairs={{2,0},{3,1},{4,2},{5,3},{6,4},{7,5},{8,6},{9,7},{10,8},{11,9},{12,... | collective-permute-start | bytes 811016 | tf_op jit(solution)/shard_map/ppermute | solution.py:89
  93.5 52.3 %collective-permute-start.6 = (f32[264,256]{1,0:T(8,128)S(1)}, f32[264,256]{1,0:T(8,128)S(1)}, u32[]{:S(2)}, u32[]{:S(2)}) collective-permute-start(f32[264,256]{1,0:T(8,128)S(1)} %get-tuple-element.11), channel_id=1, source_target_pairs={{0,2},{1,3},{2,4},{3,5},{4,6},{5,7},{6,8},{7,9},{8,10},{9,11},{10,... | collective-permute-start | bytes 811016 | tf_op jit(solution)/shard_map/ppermute | solution.py:90
  105.6 67.2 %all-to-all-start.2 = ((f32[8,26,128]{2,1,0:T(8,128)}), f32[8,26,128]{2,1,0:T(8,128)S(1)}, u32[]{:S(2)}, u32[]{:S(2)}) async-start(f32[8,26,128]{2,1,0:T(8,128)} %reshape.25), calls=%async_computation.2 | async-start | bytes 262144 | tf_op jit(solution)/shard_map/all_to_all | solution.py:276
  147.2 3.4 %collective-permute-start.7 = (f32[3,128,128]{2,1,0:T(8,128)S(1)}, f32[3,128,128]{2,1,0:T(8,128)S(1)}, u32[]{:S(2)}, u32[]{:S(2)}) collective-permute-start(f32[3,128,128]{2,1,0:T(8,128)S(1)} %get-tuple-element.15), channel_id=1, source_target_pairs={{0,1},{1,0},{2,3},{3,2},{4,5},{5,4},{6,7},{7,6},{8,9},{9,8},{10,11... | collective-permute-start | bytes 589832 | tf_op jit(solution)/shard_map/ppermute | solution.py:94
  150.6 0.9 copy-start.5
  152.8 3.1 %collective-permute-start.9 = (f32[8,128]{1,0:T(8,128)S(1)}, f32[8,128]{1,0:T(8,128)S(1)}, u32[]{:S(2)}, u32[]{:S(2)}) collective-permute-start(f32[8,128]{1,0:T(8,128)S(1)} %broadcast_in_dim.21), channel_id=1, source_target_pairs={{0,1},{1,0},{2,3},{3,2},{4,5},{5,4},{6,7},{7,6},{8,9},{9,8},{10,11... | collective-permute-start | bytes 12296 | tf_op jit(solution)/shard_map/ppermute | solution.py:289
  251.9 6.4 %collective-permute-start.10 = (f32[4,105,8,128]{3,2,1,0:T(8,128)S(1)}, f32[4,105,8,128]{3,2,1,0:T(8,128)S(1)}, u32[]{:S(2)}, u32[]{:S(2)}) collective-permute-start(f32[4,105,8,128]{3,2,1,0:T(8,128)S(1)} %all_to_all.33.own), channel_id=1, source_target_pairs={{0,1},{1,0},{2,3},{3,2},{4,5},{5,4},{6,7},{7,6},{8,9},{9,8},{10,11... | collective-permute-start | bytes 5160968 | tf_op jit(solution)/shard_map/ppermute | solution.py:302
  255.1 3.2 %copy-start.1 = (bf16[2,6,256,256]{3,2,1,0:T(8,128)(2,1)S(1)}, bf16[2,6,256,256]{3,2,1,0:T(8,128)(2,1)}, u32[]{:S(2)}) copy-start(bf16[2,6,256,256]{3,2,1,0:T(8,128)(2,1)} %probe.3) | copy-start | bytes 4718596
